TPU v7x, 8 devices: a whole 2x2x1 slice. The times are simulated.
8 devices in a mesh: grp: 1 (over z), dz: 2 (over y), dy: 2 (over x), dx: 2 (over core).
Axes of the slice: x: 2, y: 2, z: 1, core: 2. Of those that a mesh axis runs over, the one named last changes fastest.
Arguments:
- x_in: bfloat16 [8192, 7168], P(('grp', 'dx', 'dz'), 'dy')
- w_gate: bfloat16 [7168, 20480], P('dy', ('dz', 'dx'))
- w_up: bfloat16 [7168, 20480], P('dy', ('dz', 'dx'))
- w_down: bfloat16 [20480, 7168], P('dz', ('dy', 'dx'))
Outputs:
- output: bfloat16 [8192, 7168], P(('grp', 'dx', 'dz'), 'dy')
All inputs are finite; a program needn't handle non-finite values.
Results may differ from a plain program's by a relative error of at most 0.0124753.
Values are sent between devices in bfloat16 or wider.
A program may use at most 1 GiB of HBM per device.

v0:
```python
import jax
import jax.numpy as jnp
from jax import lax
from jax.sharding import PartitionSpec as P


def solution(mesh):
    x_spec = P(("grp", "dx", "dz"), "dy")
    w_in_spec = P("dy", ("dz", "dx"))
    w_out_spec = P("dz", ("dy", "dx"))

    def local_mlp(x_blk, wg_blk, wu_blk, wd_blk):
        x_rows = lax.all_gather(x_blk, "dz", axis=0, tiled=True)
        wg_cols = lax.all_gather(wg_blk, "dx", axis=1, tiled=True)
        wu_cols = lax.all_gather(wu_blk, "dx", axis=1, tiled=True)
        gate_part = jnp.dot(x_rows, wg_cols, preferred_element_type=jnp.float32)
        up_part = jnp.dot(x_rows, wu_cols, preferred_element_type=jnp.float32)
        gate_sum = lax.psum_scatter(gate_part, "dy", scatter_dimension=0, tiled=True)
        up_sum = lax.psum_scatter(up_part, "dy", scatter_dimension=0, tiled=True)
        gate_val = gate_sum.astype(jnp.bfloat16).astype(jnp.float32)
        up_val = up_sum.astype(jnp.bfloat16).astype(jnp.float32)
        hidden = (jax.nn.silu(gate_val) * up_val).astype(jnp.bfloat16)
        h_rows = lax.all_gather(hidden, "dy", axis=0, tiled=True)
        wd_cols = lax.all_gather(wd_blk, "dx", axis=1, tiled=True)
        out_part = jnp.dot(h_rows, wd_cols, preferred_element_type=jnp.float32)
        out_sum = lax.psum_scatter(out_part, "dz", scatter_dimension=0, tiled=True)
        return out_sum.astype(jnp.bfloat16)

    return jax.shard_map(local_mlp, mesh=mesh, in_specs=(x_spec, w_in_spec, w_in_spec, w_out_spec), out_specs=x_spec, check_vma=False)
```

profile of v0, /device:TPU:0, one launch (start us, length us, event | category | flops | bytes accessed | tf_op | source)
XLA Modules:
  0.0 6419.0 jit_solution(14899972749206331158)
XLA Ops:
  6.5 0.0 all-gather.6.cloned.1.call-start
  6.5 0.7 all-gather.6.cloned.1.call-update
  7.3 0.0 all-gather.8.cloned.1.call-start
  7.3 0.7 all-gather.8.cloned.1.call-update
  8.0 0.0 all-gather.10.cloned.1.call-start
  8.1 0.7 all-gather.10.cloned.1.call-update
  8.7 0.0 reduce-scatter.10.cloned.1.call-start
  8.8 342.3 %all-gather.6.cloned.1.call-done = bf16[4096,3584]{1,0:T(8,128)(2,1)} async-done(((bf16[2048,3584]{1,0:T(8,128)(2,1)}), bf16[4096,3584]{1,0:T(8,128)(2,1)}) %all-gather.6.cloned.1.call-update) | async-done | bytes 29360144 | tf_op jit(solution)/shard_map/all_gather | solution.py:13
  351.1 100.1 %all-gather.8.cloned.1.call-done = bf16[3584,10240]{1,0:T(8,128)(2,1)} async-done(((bf16[3584,5120]{1,0:T(8,128)(2,1)}), bf16[3584,10240]{1,0:T(8,128)(2,1)}) %all-gather.8.cloned.1.call-update) | async-done | bytes 73400336 | tf_op jit(solution)/shard_map/all_gather | solution.py:14
  451.2 320.6 %fusion.5 = f32[4096,10240]{1,0:T(8,128)} fusion(bf16[4096,3584]{1,0:T(8,128)(2,1)} %all-gather.6.cloned.1.call-done, bf16[3584,10240]{1,0:T(8,128)(2,1)} %all-gather.8.cloned.1.call-done), kind=kOutput, calls=%fused_computation.7 | convolution fusion | flops 300647710720 | bytes 270532608 | tf_op jit(solution)/shard_map/dot_general | solution.py:16
  771.7 0.0 reduce-scatter.10.cloned.1.call-update
  771.8 0.0 reduce-scatter.12.cloned.1.call-start
  771.8 0.0 all-gather.10.cloned.1.call-done
  771.8 320.7 %fusion.6 = f32[4096,10240]{1,0:T(8,128)} fusion(bf16[4096,3584]{1,0:T(8,128)(2,1)} %all-gather.6.cloned.1.call-done, bf16[3584,10240]{1,0:T(8,128)(2,1)} %all-gather.10.cloned.1.call-done), kind=kOutput, calls=%fused_computation.8 | convolution fusion | flops 300647710720 | bytes 270532608 | tf_op jit(solution)/shard_map/dot_general | solution.py:17
  1092.6 0.0 reduce-scatter.12.cloned.1.call-update
  1092.6 0.0 all-gather.14.cloned.1.call-start
  1092.6 0.5 all-gather.14.cloned.1.call-update
  1093.2 0.0 all-gather.12.cloned.1.call-start
  1093.2 1484.2 %reduce-scatter.10.cloned.1.call-done = f32[2048,10240]{1,0:T(8,128)} async-done(((f32[4096,10240]{1,0:T(8,128)}), f32[2048,10240]{1,0:T(8,128)}) %reduce-scatter.10.cloned.1.call-update) | async-done | bytes 83886096
  2577.4 1806.5 %reduce-scatter.12.cloned.1.call-done = f32[2048,10240]{1,0:T(8,128)} async-done(((f32[4096,10240]{1,0:T(8,128)}), f32[2048,10240]{1,0:T(8,128)}) %reduce-scatter.12.cloned.1.call-update) | async-done | bytes 83886096
  4384.0 65.2 %fusion.4 = bf16[2048,10240]{1,0:T(8,128)(2,1)} fusion(f32[2048,10240]{1,0:T(8,128)} %reduce-scatter.12.cloned.1.call-done, f32[2048,10240]{1,0:T(8,128)} %reduce-scatter.10.cloned.1.call-done), kind=kLoop, calls=%fused_computation.6 | loop fusion | flops 209715200 | bytes 209715200 | tf_op jit(solution)/shard_map/convert_element_type | solution.py:22
  4449.1 0.0 all-gather.12.cloned.1.call-update
  4449.1 0.2 reduce-scatter.14.cloned.1.call-start
  4449.4 34.6 all-gather.14.cloned.1.call-done
  4483.9 954.7 %all-gather.12.cloned.1.call-done = bf16[4096,10240]{1,0:T(8,128)(2,1)} async-done(((bf16[2048,10240]{1,0:T(8,128)(2,1)}), bf16[4096,10240]{1,0:T(8,128)(2,1)}) %all-gather.12.cloned.1.call-update) | async-done | bytes 83886096 | tf_op jit(solution)/shard_map/all_gather | solution.py:23
  5438.6 320.9 %fusion.7 = f32[4096,3584]{1,0:T(8,128)} fusion(bf16[4096,10240]{1,0:T(8,128)(2,1)} %all-gather.12.cloned.1.call-done, bf16[10240,3584]{1,0:T(8,128)(2,1)} %all-gather.14.cloned.1.call-done), kind=kOutput, calls=%fused_computation.9 | convolution fusion | flops 300647710720 | bytes 216006656 | tf_op jit(solution)/shard_map/dot_general | solution.py:25
  5759.5 0.0 reduce-scatter.14.cloned.1.call-update
  5759.5 636.3 %reduce-scatter.14.cloned.1.call-done = f32[2048,3584]{1,0:T(8,128)} async-done(((f32[4096,3584]{1,0:T(8,128)}), f32[2048,3584]{1,0:T(8,128)}) %reduce-scatter.14.cloned.1.call-update) | async-done | bytes 29360144
  6395.9 16.3 convert_element_type.23
Async XLA Ops:
  6.5 344.6 %all-gather.6.cloned.1.call-start = ((), (), s32[]{:S(2)}) async-start(), calls=%async_computation.3 | async-start | bytes 44040192 | tf_op jit(solution)/shard_map/all_gather | solution.py:13
  7.3 443.9 %all-gather.8.cloned.1.call-start = ((), (), s32[]{:S(2)}) async-start(), calls=%async_computation.4 | async-start | bytes 110100480 | tf_op jit(solution)/shard_map/all_gather | solution.py:14
  8.0 763.8 %all-gather.10.cloned.1.call-start = ((), (), s32[]{:S(2)}) async-start(), calls=%async_computation.5 | async-start | bytes 110100480 | tf_op jit(solution)/shard_map/all_gather | solution.py:15
  8.7 2568.7 %reduce-scatter.10.cloned.1.call-start = ((), (), s32[]{:S(2)}) async-start(), calls=%async_computation.8 | async-start | bytes 251658240
  771.8 3612.2 %reduce-scatter.12.cloned.1.call-start = ((), (), s32[]{:S(2)}) async-start(), calls=%async_computation.9 | async-start | bytes 251658240
  1092.6 3391.4 %all-gather.14.cloned.1.call-start = ((), (), s32[]{:S(2)}) async-start(), calls=%async_computation.7 | async-start | bytes 110100480 | tf_op jit(solution)/shard_map/all_gather | solution.py:24
  1093.2 4345.5 %all-gather.12.cloned.1.call-start = ((), (), s32[]{:S(2)}) async-start(), calls=%async_computation.6 | async-start | bytes 125829120 | tf_op jit(solution)/shard_map/all_gather | solution.py:23
  4449.1 1946.7 %reduce-scatter.14.cloned.1.call-start = ((), (), s32[]{:S(2)}) async-start(), calls=%async_computation.10 | async-start | bytes 88080384
Sparse Core Ops, SparseCore 0:
  8.9 342.2 all-gather.5
  352.6 98.5 all-gather.7
  452.7 99.6 all-gather.9
  771.9 1805.5 reduce-scatter.9
  2579.6 1804.3 reduce-scatter.11
  4385.3 98.5 all-gather.13
  4485.5 953.1 all-gather.11
  5759.7 636.1 reduce-scatter.13
where the time goes:
time: 6420 us
  waiting for transfers between devices  5360 us (83%)
  matrix products  962 us (15%)
  other arithmetic  81.5 us (1%)
    unnamed x11, waiting for transfers between devices  3930 us
    all_gather x1, waiting for transfers between devices, local_mlp(): h_rows = lax.all_gather(hidden, 'dy', axis=0, tiled=True)  955 us
    all_gather x1, waiting for transfers between devices, local_mlp(): x_rows = lax.all_gather(x_blk, 'dz', axis=0, tiled=True)  342 us
    dot_general x1, matrix products, local_mlp(): out_part = jnp.dot(h_rows, wd_cols, preferred_element_type=jnp.float32)  321 us
    dot_general x1, matrix products, local_mlp(): up_part = jnp.dot(x_rows, wu_cols, preferred_element_type=jnp.float32)  321 us
    dot_general x1, matrix products, local_mlp(): gate_part = jnp.dot(x_rows, wg_cols, preferred_element_type=jnp.float32)  321 us
  transfers between devices with their start and end apart: 8, of which 7 were waited for; matrix products, arithmetic and copies ran while one was open for 11% of the time, Pallas kernels for 0%

commit v1 on v0

v1 whole, which is shorter than its diff:
```python
import jax
import jax.numpy as jnp
from jax import lax
from jax.sharding import PartitionSpec as P


CHUNKS = 4


def solution(mesh):
    x_spec = P(("grp", "dx", "dz"), "dy")
    w_in_spec = P("dy", ("dz", "dx"))
    w_out_spec = P("dz", ("dy", "dx"))

    def swap(arr, axis):
        return lax.ppermute(arr, axis, [(0, 1), (1, 0)])

    def dot(lhs, rhs):
        return jnp.dot(lhs, rhs, preferred_element_type=jnp.float32)

    def body(x_blk, wg_blk, wu_blk, wd_blk):
        my_y = lax.axis_index("dy")
        my_c = lax.axis_index("dx")
        rows = x_blk.shape[0] // CHUNKS
        cols = wg_blk.shape[1] // 2
        n = 2 * CHUNKS

        def half(w_blk, which):
            return lax.dynamic_slice_in_dim(w_blk, which * cols, cols, axis=1)

        x_own = [x_blk[i * rows:(i + 1) * rows] for i in range(CHUNKS)]
        x_own_far = [swap(x_own[i], "dy") for i in range(CHUNKS)]
        x_oth = swap(x_blk, "dz")
        x_oth_far = [swap(x_own_far[i], "dz") for i in range(CHUNKS)]
        g_far = swap(half(wg_blk, 1 - my_y), "dy")
        u_far = swap(half(wu_blk, 1 - my_y), "dy")
        g_near = half(wg_blk, my_y)
        u_near = half(wu_blk, my_y)
        g_near = [g_near, swap(g_near, "dx")]
        u_near = [u_near, swap(u_near, "dx")]
        g_far = [g_far, swap(g_far, "dx")]
        u_far = [u_far, swap(u_far, "dx")]

        wd_all = lax.all_gather(wd_blk, "dx", axis=1, tiled=True)
        wd4 = wd_all.reshape(2, 2, cols, wd_all.shape[1])
        wd4 = jnp.where(my_c == 1, lax.rev(wd4, (0,)), wd4)
        wd4 = jnp.where(my_y == 1, lax.rev(wd4, (1,)), wd4)
        wd_perm = wd4.reshape(wd_all.shape)

        far = x_oth_far + x_own_far
        parts = {}
        for s, near in (("o", x_oth), ("m", x_blk)):
            for w, near_w in (("g", g_near), ("u", u_near)):
                for j in range(2):
                    parts[w, s, j] = dot(near, near_w[j])

        def part(w, i, j):
            r = (i % CHUNKS) * rows
            return parts[w, "o" if i < CHUNKS else "m", j][r:r + rows]

        gates, hidden, hidden_far = {}, {}, {}
        for i in range(n):
            for j in range(2):
                gates[i, j] = (part("g", i, j) + dot(far[i], g_far[j])).astype(jnp.bfloat16)
                up = (part("u", i, j) + dot(far[i], u_far[j])).astype(jnp.bfloat16).astype(jnp.float32)
                gate = gates[i, j].astype(jnp.float32)
                hidden[i, j] = (jax.nn.silu(gate) * up).astype(jnp.bfloat16)
                hidden_far[i, j] = swap(hidden[i, j], "dy")

        z_from = []
        out = jnp.zeros(x_blk.shape, jnp.bfloat16)
        for i in range(n):
            pieces = [hidden[i, 0], hidden_far[i, 0], hidden[i, 1], hidden_far[i, 1]]
            z_part = dot(jnp.concatenate(pieces, axis=1), wd_perm)
            if i >= CHUNKS:
                z_part = (z_part + z_from[i - CHUNKS]).astype(jnp.bfloat16)
            if i < CHUNKS:
                z_from.append(swap(z_part, "dz"))
            else:
                out = lax.dynamic_update_slice(out, z_part, ((i - CHUNKS) * rows, 0))
        return out

    return jax.shard_map(body, mesh=mesh, in_specs=(x_spec, w_in_spec, w_in_spec, w_out_spec),
                         out_specs=x_spec, check_vma=False)
```

time: 6420 us -> 3020 us (0.47)
  waiting for transfers between devices: 5360 us -> 1340 us
  matrix products: 962 us -> 1400 us
  local copies, waits for them, and re-layouts: 0 us -> 87.3 us
    unnamed x11 -> x1, waiting for transfers between devices: 3930 us -> 0.71 us
    all_gather x5 -> x1, waiting for transfers between devices: 1430 us -> 0.01 us  [body(): wd_all = lax.all_gather(wd_blk, 'dx', axis=1, tiled=True)]
    ppermute x0 -> x35, waiting for transfers between devices: none -> 1340 us  [swap(): return lax.ppermute(arr, axis, [(0, 1), (1, 0)])]
    dot_general x3 -> x48, matrix products: 962 us -> 1400 us  [dot(): return jnp.dot(lhs, rhs, preferred_element_type=jnp.float32)]
    select_n x0 -> x2, other arithmetic: none -> 144 us  [the longest x1 71.9 us: body(): wd4 = jnp.where(my_y == 1, lax.rev(wd4, (1,)), wd4)]
    convert_element_type x2 -> x0, other arithmetic: 81.5 us -> none  [the longest x1 65.2 us: local_mlp(): hidden = (jax.nn.silu(gate_val) * up_val).astype(jnp.bfloat16)]
    dynamic_slice x0 -> x2, local copies, waits for them, and re-layouts: none -> 66.6 us  [half(): return lax.dynamic_slice_in_dim(w_blk, which * cols, cols, axis=1)]
  transfers between devices with their start and end apart: 8 -> 36, of which waited for: 7 -> 14; matrix products, arithmetic and copies ran while one was open for 11% -> 52% of each run, Pallas kernels for 0% -> 0%
where the time goes in v1:
time: 3020 us; the launch traced here: 3010 us
  matrix products  1400 us (46%)
  waiting for transfers between devices  1340 us (44%)
  other arithmetic  144 us (5%)
  local copies, waits for them, and re-layouts  87.3 us (3%)
    dot_general x48, matrix products, dot(): return jnp.dot(lhs, rhs, preferred_element_type=jnp.float32)  1400 us
    ppermute x35, waiting for transfers between devices, swap(): return lax.ppermute(arr, axis, [(0, 1), (1, 0)])  1340 us
    select_n x1, other arithmetic, body(): wd4 = jnp.where(my_y == 1, lax.rev(wd4, (1,)), wd4)  71.9 us
    select_n x1, other arithmetic, body(): wd4 = jnp.where(my_c == 1, lax.rev(wd4, (0,)), wd4)  71.7 us
    dynamic_slice x2, local copies, waits for them, and re-layouts, half(): return lax.dynamic_slice_in_dim(w_blk, which * cols, cols, axis=1)  66.6 us
  transfers between devices with their start and end apart: 36, of which 14 were waited for; matrix products, arithmetic and copies ran while one was open for 52% of the time, Pallas kernels for 0%

profile of v1, /device:TPU:0, one launch (start us, length us, event | category | flops | bytes accessed | tf_op | source)
XLA Modules:
  0.0 3011.8 jit_solution(10549160560124842258)
XLA Ops:
  25.6 37.2 %constant_dynamic-slice_fusion.2 = (bf16[3584,2560]{1,0:T(8,128)(2,1)}, bf16[3584,2560]{1,0:T(8,128)(2,1)}) fusion(bf16[3584,5120]{1,0:T(8,128)(2,1)} %param.5, s32[]{:T(128)S(6)} %select_n.23, s32[]{:T(128)S(6)} %select_n.22), kind=kLoop, calls=%fused_computation.259 | loop fusion | bytes 73400328 | tf_op jit(solution)/shard_map/dynamic_slice | solution.py:29
  63.8 29.4 constant_dynamic-slice_fusion.1
  94.2 47.0 %convolution_bitcast_fusion.7 = f32[2048,2560]{0,1:T(8,128)} fusion(bf16[3584,2560]{1,0:T(8,128)(2,1)} %get-tuple-element.8, bf16[2048,3584]{1,0:T(8,128)(2,1)} %param.4), kind=kOutput, calls=%fused_computation.9 | convolution fusion | flops 37580963840 | bytes 54001664 | tf_op jit(solution)/shard_map/dot_general | solution.py:19
  141.3 47.2 %convolution_bitcast_fusion.6 = f32[2048,2560]{0,1:T(8,128)} fusion(bf16[3584,2560]{1,0:T(8,128)(2,1)} %get-tuple-element.5, bf16[2048,3584]{1,0:T(8,128)(2,1)} %param.4), kind=kOutput, calls=%fused_computation.8 | convolution fusion | flops 37580963840 | bytes 54001664 | tf_op jit(solution)/shard_map/dot_general | solution.py:19
  188.5 137.7 %collective-permute-done.9 = bf16[2048,3584]{1,0:T(8,128)(2,1)} collective-permute-done((bf16[2048,3584]{1,0:T(8,128)(2,1)}, bf16[2048,3584]{1,0:T(8,128)(2,1)}, u32[]{:S(2)}, u32[]{:S(2)}) %collective-permute-start.9) | collective-permute-done | bytes 14680096 | tf_op jit(solution)/shard_map/ppermute | solution.py:16
  327.9 47.4 %convolution_bitcast_fusion.3 = f32[2048,2560]{0,1:T(8,128)} fusion(bf16[3584,2560]{1,0:T(8,128)(2,1)} %get-tuple-element.8, bf16[2048,3584]{1,0:T(8,128)(2,1)} %collective-permute-done.9), kind=kOutput, calls=%fused_computation.5 | convolution fusion | flops 37580963840 | bytes 54001664 | tf_op jit(solution)/shard_map/dot_general | solution.py:19
  375.3 47.2 %convolution_bitcast_fusion.2 = f32[2048,2560]{0,1:T(8,128)} fusion(bf16[3584,2560]{1,0:T(8,128)(2,1)} %get-tuple-element.5, bf16[2048,3584]{1,0:T(8,128)(2,1)} %collective-permute-done.9), kind=kOutput, calls=%fused_computation.4 | convolution fusion | flops 37580963840 | bytes 54001664 | tf_op jit(solution)/shard_map/dot_general | solution.py:19
  422.6 547.7 %collective-permute-done.14 = bf16[512,3584]{1,0:T(8,128)(2,1)} collective-permute-done((bf16[512,3584]{1,0:T(8,128)(2,1)}, bf16[512,3584]{1,0:T(8,128)(2,1)}, u32[]{:S(2)}, u32[]{:S(2)}) %collective-permute-start.14) | collective-permute-done | bytes 3670048 | tf_op jit(solution)/shard_map/ppermute | solution.py:16
  1005.8 46.8 %collective-permute-done.1 = bf16[512,3584]{1,0:T(8,128)(2,1)S(1)} collective-permute-done((bf16[512,3584]{1,0:T(8,128)(2,1)}, bf16[512,3584]{1,0:T(8,128)(2,1)S(1)}, u32[]{:S(2)}, u32[]{:S(2)}) %collective-permute-start.1) | collective-permute-done | bytes 3670048 | tf_op jit(solution)/shard_map/ppermute | solution.py:16
  1052.7 76.0 %collective-permute-done.21 = bf16[512,3584]{1,0:T(8,128)(2,1)S(1)} collective-permute-done((bf16[512,3584]{1,0:T(8,128)(2,1)}, bf16[512,3584]{1,0:T(8,128)(2,1)S(1)}, u32[]{:S(2)}, u32[]{:S(2)}) %collective-permute-start.21) | collective-permute-done | bytes 3670048 | tf_op jit(solution)/shard_map/ppermute | solution.py:16
  1183.6 62.0 %collective-permute-done.24 = bf16[512,3584]{1,0:T(8,128)(2,1)} collective-permute-done((bf16[512,3584]{1,0:T(8,128)(2,1)S(1)}, bf16[512,3584]{1,0:T(8,128)(2,1)}, u32[]{:S(2)}, u32[]{:S(2)}) %collective-permute-start.24) | collective-permute-done | bytes 3670048 | tf_op jit(solution)/shard_map/ppermute | solution.py:16
  1280.3 43.4 %collective-permute-done.10 = bf16[512,3584]{1,0:T(8,128)(2,1)} collective-permute-done((bf16[512,3584]{1,0:T(8,128)(2,1)S(1)}, bf16[512,3584]{1,0:T(8,128)(2,1)}, u32[]{:S(2)}, u32[]{:S(2)}) %collective-permute-start.10) | collective-permute-done | bytes 3670048 | tf_op jit(solution)/shard_map/ppermute | solution.py:16
  1444.8 47.5 %convolution_bitcast_fusion.1 = f32[2048,2560]{0,1:T(8,128)} fusion(bf16[3584,2560]{1,0:T(8,128)(2,1)} %collective-permute-done.4, bf16[2048,3584]{1,0:T(8,128)(2,1)} %collective-permute-done.9), kind=kOutput, calls=%fused_computation.3 | convolution fusion | flops 37580963840 | bytes 54001664 | tf_op jit(solution)/shard_map/dot_general | solution.py:19
  1527.8 47.2 %convolution_bitcast_fusion.5 = f32[2048,2560]{0,1:T(8,128)} fusion(bf16[3584,2560]{1,0:T(8,128)(2,1)} %collective-permute-done.4, bf16[2048,3584]{1,0:T(8,128)(2,1)} %param.4), kind=kOutput, calls=%fused_computation.7 | convolution fusion | flops 37580963840 | bytes 54001664 | tf_op jit(solution)/shard_map/dot_general | solution.py:19
  1576.5 47.4 %convolution_bitcast_fusion = f32[2048,2560]{0,1:T(8,128)} fusion(bf16[3584,2560]{1,0:T(8,128)(2,1)} %collective-permute-done.6, bf16[2048,3584]{1,0:T(8,128)(2,1)} %collective-permute-done.9), kind=kOutput, calls=%fused_computation.2 | convolution fusion | flops 37580963840 | bytes 54001664 | tf_op jit(solution)/shard_map/dot_general | solution.py:19
  1623.9 47.2 %convolution_bitcast_fusion.4 = f32[2048,2560]{0,1:T(8,128)} fusion(bf16[3584,2560]{1,0:T(8,128)(2,1)} %collective-permute-done.6, bf16[2048,3584]{1,0:T(8,128)(2,1)} %param.4), kind=kOutput, calls=%fused_computation.6 | convolution fusion | flops 37580963840 | bytes 54001664 | tf_op jit(solution)/shard_map/dot_general | solution.py:19
  1941.3 71.7 %reverse_select_fusion.1 = bf16[2,2,2560,3584]{3,2,1,0:T(8,128)(2,1)} fusion(bf16[2,2,2560,3584]{3,2,1,0:T(8,128)(2,1)} %bitcast.8, pred[]{:T(512)S(6)} %eq.7), kind=kLoop, calls=%fused_computation.1 | loop fusion | flops 36700160 | bytes 146800640 | tf_op jit(solution)/shard_map/jit(_where)/select_n | solution.py:46
  2013.0 71.9 %reverse_select_fusion = bf16[2,2,2560,3584]{3,2,1,0:T(8,128)(2,1)} fusion(bf16[2,2,2560,3584]{3,2,1,0:T(8,128)(2,1)} %reverse_select_fusion.1, pred[]{:T(512)S(6)} %eq.6), kind=kLoop, calls=%fused_computation | loop fusion | flops 36700160 | bytes 146800640 | tf_op jit(solution)/shard_map/jit(_where)/select_n | solution.py:47
  2087.0 58.1 %fusion.8 = f32[512,3584]{1,0:T(8,128)} fusion(bf16[10240,3584]{1,0:T(8,128)(2,1)} %bitcast.9, bf16[512,2560]{0,1:T(8,128)(2,1)} %collective-permute-done.12, bf16[512,2560]{0,1:T(8,128)(2,1)} %fusion.189, bf16[512,2560]{0,1:T(8,128)(2,1)} %collective-permute-done.11, bf16[512,2560]{0,1:T(8,128)(2,1)} %fusion.190), kind=kOutput, calls=%fused_computation.18 | convolution fusion | flops 37622906880 | bytes 91226112 | tf_op jit(solution)/shard_map/dot_general | solution.py:19
  2145.8 55.4 %collective-permute-done.19 = bf16[512,2560]{0,1:T(8,128)(2,1)} collective-permute-done((bf16[512,2560]{0,1:T(8,128)(2,1)}, bf16[512,2560]{0,1:T(8,128)(2,1)}, u32[]{:S(2)}, u32[]{:S(2)}) %collective-permute-start.19) | collective-permute-done | bytes 2621472 | tf_op jit(solution)/shard_map/ppermute | solution.py:16
  2201.9 58.1 %fusion.24 = f32[512,3584]{1,0:T(8,128)} fusion(bf16[10240,3584]{1,0:T(8,128)(2,1)} %bitcast.9, bf16[512,2560]{0,1:T(8,128)(2,1)} %collective-permute-done.19, bf16[512,2560]{0,1:T(8,128)(2,1)} %fusion.185, bf16[512,2560]{0,1:T(8,128)(2,1)} %collective-permute-done.18, bf16[512,2560]{0,1:T(8,128)(2,1)} %fusion.186), kind=kOutput, calls=%fused_computation.34 | convolution fusion | flops 37622906880 | bytes 91226112 | tf_op jit(solution)/shard_map/dot_general | solution.py:19
  2261.3 52.2 %collective-permute-done.26 = bf16[512,2560]{0,1:T(8,128)(2,1)} collective-permute-done((bf16[512,2560]{0,1:T(8,128)(2,1)}, bf16[512,2560]{0,1:T(8,128)(2,1)}, u32[]{:S(2)}, u32[]{:S(2)}) %collective-permute-start.26) | collective-permute-done | bytes 2621472 | tf_op jit(solution)/shard_map/ppermute | solution.py:16
  2313.8 58.2 %fusion.40 = f32[512,3584]{1,0:T(8,128)} fusion(bf16[10240,3584]{1,0:T(8,128)(2,1)} %bitcast.9, bf16[512,2560]{0,1:T(8,128)(2,1)} %collective-permute-done.26, bf16[512,2560]{0,1:T(8,128)(2,1)} %fusion.181, bf16[512,2560]{0,1:T(8,128)(2,1)} %collective-permute-done.25, bf16[512,2560]{0,1:T(8,128)(2,1)} %fusion.182), kind=kOutput, calls=%fused_computation.50 | convolution fusion | flops 37622906880 | bytes 91226112 | tf_op jit(solution)/shard_map/dot_general | solution.py:19
  2374.5 59.4 %fusion.56 = f32[512,3584]{1,0:T(8,128)} fusion(bf16[10240,3584]{1,0:T(8,128)(2,1)} %bitcast.9, bf16[512,2560]{0,1:T(8,128)(2,1)} %collective-permute-done.33, bf16[512,2560]{0,1:T(8,128)(2,1)} %fusion.177, bf16[512,2560]{0,1:T(8,128)(2,1)} %collective-permute-done.32, bf16[512,2560]{0,1:T(8,128)(2,1)S(1)} %copy-done.10), kind=kOutput, calls=%fused_computation.66 | convolution fusion | flops 37622906880 | bytes 91226112 | tf_op jit(solution)/shard_map/dot_general | solution.py:19
  2435.9 38.7 %collective-permute-done.13 = f32[512,3584]{1,0:T(8,128)} collective-permute-done((f32[512,3584]{1,0:T(8,128)}, f32[512,3584]{1,0:T(8,128)}, u32[]{:S(2)}, u32[]{:S(2)}) %collective-permute-start.13) | collective-permute-done | bytes 7340064 | tf_op jit(solution)/shard_map/ppermute | solution.py:16
  2475.0 61.4 %add_convert_fusion.3 = bf16[512,3584]{1,0:T(8,128)(2,1)} fusion(f32[512,3584]{1,0:T(8,128)} %collective-permute-done.13, bf16[10240,3584]{1,0:T(8,128)(2,1)} %bitcast.9, bf16[512,2560]{0,1:T(8,128)(2,1)} %collective-permute-done.8, bf16[512,2560]{0,1:T(8,128)(2,1)} %fusion.191, bf16[512,2560]{0,1:T(8,128)(2,1)} %collective-permute-done.3, ...), kind=kOutput, calls=%fused_computation.77 | convolution fusion | flops 37626576896 | bytes 94896128 | tf_op jit(solution)/shard_map/dot_general | solution.py:19
  2551.5 80.5 %collective-permute-done.20 = f32[512,3584]{1,0:T(8,128)} collective-permute-done((f32[512,3584]{1,0:T(8,128)}, f32[512,3584]{1,0:T(8,128)}, u32[]{:S(2)}, u32[]{:S(2)}) %collective-permute-start.20) | collective-permute-done | bytes 7340064 | tf_op jit(solution)/shard_map/ppermute | solution.py:16
  2632.3 61.5 %fusion.72 = bf16[2048,3584]{1,0:T(8,128)(2,1)} fusion(bf16[2048,3584]{1,0:T(8,128)(2,1)} %dynamic_update_slice.12, f32[512,3584]{1,0:T(8,128)} %collective-permute-done.20, bf16[10240,3584]{1,0:T(8,128)(2,1)} %bitcast.9, bf16[512,2560]{0,1:T(8,128)(2,1)} %collective-permute-done.16, bf16[512,2560]{0,1:T(8,128)(2,1)} %fusion.187, ...), kind=kOutput, calls=%fused_computation.110 | convolution fusion | flops 37626576896 | bytes 94896128 | tf_op jit(solution)/shard_map/dot_general | solution.py:19
  2694.5 94.8 %collective-permute-done.27 = f32[512,3584]{1,0:T(8,128)} collective-permute-done((f32[512,3584]{1,0:T(8,128)}, f32[512,3584]{1,0:T(8,128)}, u32[]{:S(2)}, u32[]{:S(2)}) %collective-permute-start.27) | collective-permute-done | bytes 7340064 | tf_op jit(solution)/shard_map/ppermute | solution.py:16
  2789.3 61.5 %fusion.75 = bf16[2048,3584]{1,0:T(8,128)(2,1)} fusion(bf16[2048,3584]{1,0:T(8,128)(2,1)} %fusion.72, f32[512,3584]{1,0:T(8,128)} %collective-permute-done.27, bf16[10240,3584]{1,0:T(8,128)(2,1)} %bitcast.9, bf16[512,2560]{0,1:T(8,128)(2,1)} %collective-permute-done.23, bf16[512,2560]{0,1:T(8,128)(2,1)} %fusion.183, ...), kind=kOutput, calls=%fused_computation.111 | convolution fusion | flops 37626576896 | bytes 94896128 | tf_op jit(solution)/shard_map/dot_general | solution.py:19
  2850.7 91.4 %collective-permute-done.34 = f32[512,3584]{1,0:T(8,128)} collective-permute-done((f32[512,3584]{1,0:T(8,128)}, f32[512,3584]{1,0:T(8,128)}, u32[]{:S(2)}, u32[]{:S(2)}) %collective-permute-start.34) | collective-permute-done | bytes 7340064 | tf_op jit(solution)/shard_map/ppermute | solution.py:16
  2942.2 62.3 %fusion.78 = bf16[2048,3584]{1,0:T(8,128)(2,1)} fusion(bf16[2048,3584]{1,0:T(8,128)(2,1)} %fusion.75, f32[512,3584]{1,0:T(8,128)} %collective-permute-done.34, bf16[10240,3584]{1,0:T(8,128)(2,1)} %bitcast.9, bf16[512,2560]{0,1:T(8,128)(2,1)} %collective-permute-done.30, bf16[512,2560]{0,1:T(8,128)(2,1)} %fusion.179, ...), kind=kOutput, calls=%fused_computation.112 | convolution fusion | flops 37626576896 | bytes 94896128 | tf_op jit(solution)/shard_map/dot_general | solution.py:19
  (133 shorter events, 602.2 us)
Async XLA Ops:
  6.5 1934.8 %all-gather.2.cloned.1.call-start = ((), (), s32[]{:S(2)}) async-start(), calls=%async_computation | async-start | bytes 110100480 | tf_op jit(solution)/shard_map/all_gather | solution.py:44
  7.3 319.0 %collective-permute-start.9 = (bf16[2048,3584]{1,0:T(8,128)(2,1)}, bf16[2048,3584]{1,0:T(8,128)(2,1)}, u32[]{:S(2)}, u32[]{:S(2)}) collective-permute-start(bf16[2048,3584]{1,0:T(8,128)(2,1)} %param.4), channel_id=1, source_target_pairs={{0,4},{4,0},{1,5},{5,1},{2,6},{6,2},{3,7},{7,3}} | collective-permute-start | bytes 44040200 | tf_op jit(solution)/shard_map/ppermute | solution.py:16
  24.6 981.2 %collective-permute-start.28 = (bf16[512,3584]{1,0:T(8,128)(2,1)}, bf16[512,3584]{1,0:T(8,128)(2,1)}, u32[]{:S(2)}, u32[]{:S(2)}) collective-permute-start(bf16[512,3584]{1,0:T(8,128)(2,1)} %get-tuple-element.9), channel_id=1, source_target_pairs={{0,2},{2,0},{1,3},{3,1},{4,6},{6,4},{5,7},{7,5}} | collective-permute-start | bytes 11010056 | tf_op jit(solution)/shard_map/ppermute | solution.py:16
  62.8 908.9 %collective-permute-start = (bf16[3584,2560]{1,0:T(8,128)(2,1)}, bf16[3584,2560]{1,0:T(8,128)(2,1)}, u32[]{:S(2)}, u32[]{:S(2)}) collective-permute-start(bf16[3584,2560]{1,0:T(8,128)(2,1)} %get-tuple-element.7), channel_id=1, source_target_pairs={{0,2},{2,0},{1,3},{3,1},{4,6},{6,4},{5,7},{7,5}} | collective-permute-start | bytes 55050248 | tf_op jit(solution)/shard_map/ppermute | solution.py:16
  63.8 1380.5 %collective-permute-start.4 = (bf16[3584,2560]{1,0:T(8,128)(2,1)}, bf16[3584,2560]{1,0:T(8,128)(2,1)}, u32[]{:S(2)}, u32[]{:S(2)}) collective-permute-start(bf16[3584,2560]{1,0:T(8,128)(2,1)} %get-tuple-element.8), channel_id=1, source_target_pairs={{0,1},{1,0},{2,3},{3,2},{4,5},{5,4},{6,7},{7,6}} | collective-permute-start | bytes 55050248 | tf_op jit(solution)/shard_map/ppermute | solution.py:16
  93.2 894.8 %collective-permute-start.2 = (bf16[3584,2560]{1,0:T(8,128)(2,1)}, bf16[3584,2560]{1,0:T(8,128)(2,1)}, u32[]{:S(2)}, u32[]{:S(2)}) collective-permute-start(bf16[3584,2560]{1,0:T(8,128)(2,1)} %get-tuple-element.6), channel_id=1, source_target_pairs={{0,2},{2,0},{1,3},{3,1},{4,6},{6,4},{5,7},{7,5}} | collective-permute-start | bytes 55050248 | tf_op jit(solution)/shard_map/ppermute | solution.py:16
  326.2 644.0 %collective-permute-start.14 = (bf16[512,3584]{1,0:T(8,128)(2,1)}, bf16[512,3584]{1,0:T(8,128)(2,1)}, u32[]{:S(2)}, u32[]{:S(2)}) collective-permute-start(bf16[512,3584]{1,0:T(8,128)(2,1)} %get-tuple-element.10), channel_id=1, source_target_pairs={{0,2},{2,0},{1,3},{3,1},{4,6},{6,4},{5,7},{7,5}} | collective-permute-start | bytes 11010056 | tf_op jit(solution)/shard_map/ppermute | solution.py:16
  971.7 157.0 %collective-permute-start.21 = (bf16[512,3584]{1,0:T(8,128)(2,1)}, bf16[512,3584]{1,0:T(8,128)(2,1)S(1)}, u32[]{:S(2)}, u32[]{:S(2)}) collective-permute-start(bf16[512,3584]{1,0:T(8,128)(2,1)} %get-tuple-element.12), channel_id=1, source_target_pairs={{0,2},{2,0},{1,3},{3,1},{4,6},{6,4},{5,7},{7,5}} | collective-permute-start | bytes 11010056 | tf_op jit(solution)/shard_map/ppermute | solution.py:16
  987.9 587.1 %collective-permute-start.6 = (bf16[3584,2560]{1,0:T(8,128)(2,1)}, bf16[3584,2560]{1,0:T(8,128)(2,1)}, u32[]{:S(2)}, u32[]{:S(2)}) collective-permute-start(bf16[3584,2560]{1,0:T(8,128)(2,1)} %get-tuple-element.5), channel_id=1, source_target_pairs={{0,1},{1,0},{2,3},{3,2},{4,5},{5,4},{6,7},{7,6}} | collective-permute-start | bytes 55050248 | tf_op jit(solution)/shard_map/ppermute | solution.py:16
  1005.8 257.8 %collective-permute-start.17 = (bf16[512,3584]{1,0:T(8,128)(2,1)}, bf16[512,3584]{1,0:T(8,128)(2,1)S(1)}, u32[]{:S(2)}, u32[]{:S(2)}) collective-permute-start(bf16[512,3584]{1,0:T(8,128)(2,1)} %collective-permute-done.14), channel_id=1, source_target_pairs={{0,4},{4,0},{1,5},{5,1},{2,6},{6,2},{3,7},{7,3}} | collective-permute-start | bytes 11010056 | tf_op jit(solution)/shard_map/ppermute | solution.py:16
  1052.6 114.3 %collective-permute-start.31 = (bf16[512,3584]{1,0:T(8,128)(2,1)}, bf16[512,3584]{1,0:T(8,128)(2,1)}, u32[]{:S(2)}, u32[]{:S(2)}) collective-permute-start(bf16[512,3584]{1,0:T(8,128)(2,1)} %collective-permute-done.28), channel_id=1, source_target_pairs={{0,4},{4,0},{1,5},{5,1},{2,6},{6,2},{3,7},{7,3}} | collective-permute-start | bytes 11010056 | tf_op jit(solution)/shard_map/ppermute | solution.py:16
  1128.7 116.9 %collective-permute-start.24 = (bf16[512,3584]{1,0:T(8,128)(2,1)S(1)}, bf16[512,3584]{1,0:T(8,128)(2,1)}, u32[]{:S(2)}, u32[]{:S(2)}) collective-permute-start(bf16[512,3584]{1,0:T(8,128)(2,1)S(1)} %collective-permute-done.21), channel_id=1, source_target_pairs={{0,4},{4,0},{1,5},{5,1},{2,6},{6,2},{3,7},{7,3}} | collective-permute-start | bytes 11010056 | tf_op jit(solution)/shard_map/ppermute | solution.py:16
  1167.0 156.8 %collective-permute-start.10 = (bf16[512,3584]{1,0:T(8,128)(2,1)S(1)}, bf16[512,3584]{1,0:T(8,128)(2,1)}, u32[]{:S(2)}, u32[]{:S(2)}) collective-permute-start(bf16[512,3584]{1,0:T(8,128)(2,1)S(1)} %collective-permute-done.1), channel_id=1, source_target_pairs={{0,4},{4,0},{1,5},{5,1},{2,6},{6,2},{3,7},{7,3}} | collective-permute-start | bytes 11010056 | tf_op jit(solution)/shard_map/ppermute | solution.py:16
  1245.6 1188.3 %collective-permute-start.3 = (bf16[512,2560]{0,1:T(8,128)(2,1)}, bf16[512,2560]{0,1:T(8,128)(2,1)}, u32[]{:S(2)}, u32[]{:S(2)}) collective-permute-start(bf16[512,2560]{0,1:T(8,128)(2,1)} %fusion.192), channel_id=1, source_target_pairs={{0,2},{2,0},{1,3},{3,1},{4,6},{6,4},{5,7},{7,5}} | collective-permute-start | bytes 7864328 | tf_op jit(solution)/shard_map/ppermute | solution.py:16
  1263.6 1279.5 %collective-permute-start.15 = (bf16[512,2560]{0,1:T(8,128)(2,1)}, bf16[512,2560]{0,1:T(8,128)(2,1)}, u32[]{:S(2)}, u32[]{:S(2)}) collective-permute-start(bf16[512,2560]{0,1:T(8,128)(2,1)} %fusion.188), channel_id=1, source_target_pairs={{0,2},{2,0},{1,3},{3,1},{4,6},{6,4},{5,7},{7,5}} | collective-permute-start | bytes 7864328 | tf_op jit(solution)/shard_map/ppermute | solution.py:16
  1323.8 347.4 %collective-permute-start.5 = (bf16[3584,2560]{1,0:T(8,128)(2,1)}, bf16[3584,2560]{1,0:T(8,128)(2,1)}, u32[]{:S(2)}, u32[]{:S(2)}) collective-permute-start(bf16[3584,2560]{1,0:T(8,128)(2,1)} %collective-permute-done), channel_id=1, source_target_pairs={{0,1},{1,0},{2,3},{3,2},{4,5},{5,4},{6,7},{7,6}} | collective-permute-start | bytes 55050248 | tf_op jit(solution)/shard_map/ppermute | solution.py:16
  1444.3 243.1 %collective-permute-start.7 = (bf16[3584,2560]{1,0:T(8,128)(2,1)}, bf16[3584,2560]{1,0:T(8,128)(2,1)}, u32[]{:S(2)}, u32[]{:S(2)}) collective-permute-start(bf16[3584,2560]{1,0:T(8,128)(2,1)} %collective-permute-done.2), channel_id=1, source_target_pairs={{0,1},{1,0},{2,3},{3,2},{4,5},{5,4},{6,7},{7,6}} | collective-permute-start | bytes 55050248 | tf_op jit(solution)/shard_map/ppermute | solution.py:16
  1575.0 509.9 %collective-permute-start.11 = (bf16[512,2560]{0,1:T(8,128)(2,1)}, bf16[512,2560]{0,1:T(8,128)(2,1)}, u32[]{:S(2)}, u32[]{:S(2)}) collective-permute-start(bf16[512,2560]{0,1:T(8,128)(2,1)} %fusion.190), channel_id=1, source_target_pairs={{0,2},{2,0},{1,3},{3,1},{4,6},{6,4},{5,7},{7,5}} | collective-permute-start | bytes 7864328 | tf_op jit(solution)/shard_map/ppermute | solution.py:16
  1671.1 474.0 %collective-permute-start.18 = (bf16[512,2560]{0,1:T(8,128)(2,1)}, bf16[512,2560]{0,1:T(8,128)(2,1)}, u32[]{:S(2)}, u32[]{:S(2)}) collective-permute-start(bf16[512,2560]{0,1:T(8,128)(2,1)} %fusion.186), channel_id=1, source_target_pairs={{0,2},{2,0},{1,3},{3,1},{4,6},{6,4},{5,7},{7,5}} | collective-permute-start | bytes 7864328 | tf_op jit(solution)/shard_map/ppermute | solution.py:16
  1705.4 380.3 %collective-permute-start.12 = (bf16[512,2560]{0,1:T(8,128)(2,1)}, bf16[512,2560]{0,1:T(8,128)(2,1)}, u32[]{:S(2)}, u32[]{:S(2)}) collective-permute-start(bf16[512,2560]{0,1:T(8,128)(2,1)} %fusion.189), channel_id=1, source_target_pairs={{0,2},{2,0},{1,3},{3,1},{4,6},{6,4},{5,7},{7,5}} | collective-permute-start | bytes 7864328 | tf_op jit(solution)/shard_map/ppermute | solution.py:16
  2084.9 175.1 %collective-permute-start.25 = (bf16[512,2560]{0,1:T(8,128)(2,1)}, bf16[512,2560]{0,1:T(8,128)(2,1)}, u32[]{:S(2)}, u32[]{:S(2)}) collective-permute-start(bf16[512,2560]{0,1:T(8,128)(2,1)} %fusion.182), channel_id=1, source_target_pairs={{0,2},{2,0},{1,3},{3,1},{4,6},{6,4},{5,7},{7,5}} | collective-permute-start | bytes 7864328 | tf_op jit(solution)/shard_map/ppermute | solution.py:16
  2085.6 115.5 %collective-permute-start.19 = (bf16[512,2560]{0,1:T(8,128)(2,1)}, bf16[512,2560]{0,1:T(8,128)(2,1)}, u32[]{:S(2)}, u32[]{:S(2)}) collective-permute-start(bf16[512,2560]{0,1:T(8,128)(2,1)} %fusion.185), channel_id=1, source_target_pairs={{0,2},{2,0},{1,3},{3,1},{4,6},{6,4},{5,7},{7,5}} | collective-permute-start | bytes 7864328 | tf_op jit(solution)/shard_map/ppermute | solution.py:16
  2145.1 227.0 %collective-permute-start.32 = (bf16[512,2560]{0,1:T(8,128)(2,1)S(1)}, bf16[512,2560]{0,1:T(8,128)(2,1)}, u32[]{:S(2)}, u32[]{:S(2)}) collective-permute-start(bf16[512,2560]{0,1:T(8,128)(2,1)S(1)} %copy-done.10), channel_id=1, source_target_pairs={{0,2},{2,0},{1,3},{3,1},{4,6},{6,4},{5,7},{7,5}} | collective-permute-start | bytes 7864328 | tf_op jit(solution)/shard_map/ppermute | solution.py:16
  2313.5 161.2 %collective-permute-start.13 = (f32[512,3584]{1,0:T(8,128)}, f32[512,3584]{1,0:T(8,128)}, u32[]{:S(2)}, u32[]{:S(2)}) collective-permute-start(f32[512,3584]{1,0:T(8,128)} %fusion.8), channel_id=1, source_target_pairs={{0,4},{4,0},{1,5},{5,1},{2,6},{6,2},{3,7},{7,3}} | collective-permute-start | bytes 22020104 | tf_op jit(solution)/shard_map/ppermute | solution.py:16
  2372.8 259.2 %collective-permute-start.20 = (f32[512,3584]{1,0:T(8,128)}, f32[512,3584]{1,0:T(8,128)}, u32[]{:S(2)}, u32[]{:S(2)}) collective-permute-start(f32[512,3584]{1,0:T(8,128)} %fusion.24), channel_id=1, source_target_pairs={{0,4},{4,0},{1,5},{5,1},{2,6},{6,2},{3,7},{7,3}} | collective-permute-start | bytes 22020104 | tf_op jit(solution)/shard_map/ppermute | solution.py:16
  2433.9 259.9 %collective-permute-start.22 = (bf16[512,2560]{0,1:T(8,128)(2,1)}, bf16[512,2560]{0,1:T(8,128)(2,1)}, u32[]{:S(2)}, u32[]{:S(2)}) collective-permute-start(bf16[512,2560]{0,1:T(8,128)(2,1)} %fusion.184), channel_id=1, source_target_pairs={{0,2},{2,0},{1,3},{3,1},{4,6},{6,4},{5,7},{7,5}} | collective-permute-start | bytes 7864328 | tf_op jit(solution)/shard_map/ppermute | solution.py:16
  2435.2 114.9 %collective-permute-start.16 = (bf16[512,2560]{0,1:T(8,128)(2,1)}, bf16[512,2560]{0,1:T(8,128)(2,1)}, u32[]{:S(2)}, u32[]{:S(2)}) collective-permute-start(bf16[512,2560]{0,1:T(8,128)(2,1)} %fusion.187), channel_id=1, source_target_pairs={{0,2},{2,0},{1,3},{3,1},{4,6},{6,4},{5,7},{7,5}} | collective-permute-start | bytes 7864328 | tf_op jit(solution)/shard_map/ppermute | solution.py:16
  2474.7 314.6 %collective-permute-start.27 = (f32[512,3584]{1,0:T(8,128)}, f32[512,3584]{1,0:T(8,128)}, u32[]{:S(2)}, u32[]{:S(2)}) collective-permute-start(f32[512,3584]{1,0:T(8,128)} %fusion.40), channel_id=1, source_target_pairs={{0,4},{4,0},{1,5},{5,1},{2,6},{6,2},{3,7},{7,3}} | collective-permute-start | bytes 22020104 | tf_op jit(solution)/shard_map/ppermute | solution.py:16
  2543.0 307.7 %collective-permute-start.29 = (bf16[512,2560]{0,1:T(8,128)(2,1)S(1)}, bf16[512,2560]{0,1:T(8,128)(2,1)}, u32[]{:S(2)}, u32[]{:S(2)}) collective-permute-start(bf16[512,2560]{0,1:T(8,128)(2,1)S(1)} %copy-done.9), channel_id=1, source_target_pairs={{0,2},{2,0},{1,3},{3,1},{4,6},{6,4},{5,7},{7,5}} | collective-permute-start | bytes 7864328 | tf_op jit(solution)/shard_map/ppermute | solution.py:16
  2550.1 144.3 %collective-permute-start.23 = (bf16[512,2560]{0,1:T(8,128)(2,1)}, bf16[512,2560]{0,1:T(8,128)(2,1)}, u32[]{:S(2)}, u32[]{:S(2)}) collective-permute-start(bf16[512,2560]{0,1:T(8,128)(2,1)} %fusion.183), channel_id=1, source_target_pairs={{0,2},{2,0},{1,3},{3,1},{4,6},{6,4},{5,7},{7,5}} | collective-permute-start | bytes 7864328 | tf_op jit(solution)/shard_map/ppermute | solution.py:16
  2632.0 310.2 %collective-permute-start.34 = (f32[512,3584]{1,0:T(8,128)}, f32[512,3584]{1,0:T(8,128)}, u32[]{:S(2)}, u32[]{:S(2)}) collective-permute-start(f32[512,3584]{1,0:T(8,128)} %fusion.56), channel_id=1, source_target_pairs={{0,4},{4,0},{1,5},{5,1},{2,6},{6,2},{3,7},{7,3}} | collective-permute-start | bytes 22020104 | tf_op jit(solution)/shard_map/ppermute | solution.py:16
  2693.8 157.0 %collective-permute-start.30 = (bf16[512,2560]{0,1:T(8,128)(2,1)}, bf16[512,2560]{0,1:T(8,128)(2,1)}, u32[]{:S(2)}, u32[]{:S(2)}) collective-permute-start(bf16[512,2560]{0,1:T(8,128)(2,1)} %fusion.179), channel_id=1, source_target_pairs={{0,2},{2,0},{1,3},{3,1},{4,6},{6,4},{5,7},{7,5}} | collective-permute-start | bytes 7864328 | tf_op jit(solution)/shard_map/ppermute | solution.py:16
  (23 other events, 968.0 us)
Sparse Core Ops, SparseCore 0:
  8.8 129.6 all-gather.1

commit v2 on v1

--- a/solution.py
+++ b/solution.py
@@ -28,7 +28,9 @@
         def half(w_blk, which):
             return lax.dynamic_slice_in_dim(w_blk, which * cols, cols, axis=1)
 
-        x_own = [x_blk[i * rows:(i + 1) * rows] for i in range(CHUNKS)]
+        x_own = [x_blk[:rows]]
+        x_rest, _ = lax.optimization_barrier((x_blk, x_own[0]))
+        x_own += [x_rest[i * rows:(i + 1) * rows] for i in range(1, CHUNKS)]
         x_own_far = [swap(x_own[i], "dy") for i in range(CHUNKS)]
         x_oth = swap(x_blk, "dz")
         x_oth_far = [swap(x_own_far[i], "dz") for i in range(CHUNKS)]
@@ -41,7 +43,9 @@
         g_far = [g_far, swap(g_far, "dx")]
         u_far = [u_far, swap(u_far, "dx")]
 
-        wd_all = lax.all_gather(wd_blk, "dx", axis=1, tiled=True)
+        wd_other = swap(wd_blk, "dx")
+        wd_all = jnp.where(my_c == 0, jnp.concatenate([wd_blk, wd_other], axis=1),
+                           jnp.concatenate([wd_other, wd_blk], axis=1))
         wd4 = wd_all.reshape(2, 2, cols, wd_all.shape[1])
         wd4 = jnp.where(my_c == 1, lax.rev(wd4, (0,)), wd4)
         wd4 = jnp.where(my_y == 1, lax.rev(wd4, (1,)), wd4)
@@ -65,11 +69,15 @@
                 up = (part("u", i, j) + dot(far[i], u_far[j])).astype(jnp.bfloat16).astype(jnp.float32)
                 gate = gates[i, j].astype(jnp.float32)
                 hidden[i, j] = (jax.nn.silu(gate) * up).astype(jnp.bfloat16)
-                hidden_far[i, j] = swap(hidden[i, j], "dy")
+                if (i, j) == (n - 1, 1):
+                    hidden_far[i, j] = [swap(hidden[i, j][k * rows // 2:(k + 1) * rows // 2], "dy")
+                                        for k in range(2)]
+                else:
+                    hidden_far[i, j] = swap(hidden[i, j], "dy")
 
         z_from = []
         out = jnp.zeros(x_blk.shape, jnp.bfloat16)
-        for i in range(n):
+        for i in range(n - 1):
             pieces = [hidden[i, 0], hidden_far[i, 0], hidden[i, 1], hidden_far[i, 1]]
             z_part = dot(jnp.concatenate(pieces, axis=1), wd_perm)
             if i >= CHUNKS:
@@ -78,6 +86,14 @@
                 z_from.append(swap(z_part, "dz"))
             else:
                 out = lax.dynamic_update_slice(out, z_part, ((i - CHUNKS) * rows, 0))
+        i = n - 1
+        z_part = dot(hidden[i, 1], wd_perm[2 * cols:3 * cols]) + z_from[CHUNKS - 1]
+        z_part = dot(hidden[i, 0], wd_perm[:cols]) + z_part
+        z_part = dot(hidden_far[i, 0], wd_perm[cols:2 * cols]) + z_part
+        for k in range(2):
+            z_half = dot(hidden_far[i, 1][k], wd_perm[3 * cols:]) + z_part[k * rows // 2:(k + 1) * rows // 2]
+            z_half = z_half.astype(jnp.bfloat16)
+            out = lax.dynamic_update_slice(out, z_half, ((CHUNKS - 1) * rows + k * rows // 2, 0))
         return out
 
     return jax.shard_map(body, mesh=mesh, in_specs=(x_spec, w_in_spec, w_in_spec, w_out_spec),

time: 3020 us -> 2940 us (0.974)
  waiting for transfers between devices: 1340 us -> 1180 us
  other arithmetic: 144 us -> 215 us
    ppermute x35 -> x37, waiting for transfers between devices: 1340 us -> 1180 us  [swap(): return lax.ppermute(arr, axis, [(0, 1), (1, 0)])]
    select_n x0 -> x1, other arithmetic: none -> 71.3 us  [body(): jnp.where(my_c == 0, jnp.concatenate([wd_blk, wd_other], axis=1), jnp.con...]
    dot_general x48 -> x52, matrix products: 1400 us -> 1430 us  [dot(): return jnp.dot(lhs, rhs, preferred_element_type=jnp.float32)]
  transfers between devices with their start and end apart: 36 -> 37, of which waited for: 14 -> 13; matrix products, arithmetic and copies ran while one was open for 52% -> 58% of each run, Pallas kernels for 0% -> 0%
where the time goes in v2:
time: 2940 us; the launch traced here: 2930 us
  matrix products  1430 us (49%)
  waiting for transfers between devices  1180 us (40%)
  other arithmetic  215 us (7%)
  local copies, waits for them, and re-layouts  73 us (2%)
  starting transfers between devices  35.8 us (1%)
    dot_general x52, matrix products, dot(): return jnp.dot(lhs, rhs, preferred_element_type=jnp.float32)  1430 us
    ppermute x37, waiting for transfers between devices, swap(): return lax.ppermute(arr, axis, [(0, 1), (1, 0)])  1180 us
    select_n x1, other arithmetic, body(): wd4 = jnp.where(my_y == 1, lax.rev(wd4, (1,)), wd4)  71.9 us
    select_n x1, other arithmetic, body(): wd4 = jnp.where(my_c == 1, lax.rev(wd4, (0,)), wd4)  71.8 us
    select_n x1, other arithmetic, body(): jnp.where(my_c == 0, jnp.concatenate([wd_blk, wd_other], axis=1), jnp.con...  71.3 us
  transfers between devices with their start and end apart: 37, of which 13 were waited for; matrix products, arithmetic and copies ran while one was open for 58% of the time, Pallas kernels for 0%

profile of v2, /device:TPU:0, one launch (start us, length us, event | category | flops | bytes accessed | tf_op | source)
XLA Modules:
  0.0 2928.7 jit_solution(15611609783657811792)
XLA Ops:
  17.4 26.4 constant_dynamic-slice_fusion.2
  45.2 26.4 constant_dynamic-slice_fusion.1
  71.6 47.0 %convolution_bitcast_fusion.7 = f32[2048,2560]{0,1:T(8,128)} fusion(bf16[3584,2560]{1,0:T(8,128)(2,1)} %get-tuple-element.10, bf16[2048,3584]{1,0:T(8,128)(2,1)} %param.4), kind=kOutput, calls=%fused_computation.20 | convolution fusion | flops 37580963840 | bytes 54001664 | tf_op jit(solution)/shard_map/dot_general | solution.py:19
  118.6 47.4 %convolution_bitcast_fusion.6 = f32[2048,2560]{0,1:T(8,128)} fusion(bf16[3584,2560]{1,0:T(8,128)(2,1)} %get-tuple-element.7, bf16[2048,3584]{1,0:T(8,128)(2,1)} %param.4), kind=kOutput, calls=%fused_computation.19 | convolution fusion | flops 37580963840 | bytes 54001664 | tf_op jit(solution)/shard_map/dot_general | solution.py:19
  166.0 152.9 %collective-permute-done.10 = bf16[2048,3584]{1,0:T(8,128)(2,1)} collective-permute-done((bf16[2048,3584]{1,0:T(8,128)(2,1)}, bf16[2048,3584]{1,0:T(8,128)(2,1)}, u32[]{:S(2)}, u32[]{:S(2)}) %collective-permute-start.10) | collective-permute-done | bytes 14680096 | tf_op jit(solution)/shard_map/ppermute | solution.py:16
  320.6 47.4 %convolution_bitcast_fusion.3 = f32[2048,2560]{0,1:T(8,128)} fusion(bf16[3584,2560]{1,0:T(8,128)(2,1)} %get-tuple-element.10, bf16[2048,3584]{1,0:T(8,128)(2,1)} %collective-permute-done.10), kind=kOutput, calls=%fused_computation.16 | convolution fusion | flops 37580963840 | bytes 54001664 | tf_op jit(solution)/shard_map/dot_general | solution.py:19
  368.0 47.5 %convolution_bitcast_fusion.2 = f32[2048,2560]{0,1:T(8,128)} fusion(bf16[3584,2560]{1,0:T(8,128)(2,1)} %get-tuple-element.7, bf16[2048,3584]{1,0:T(8,128)(2,1)} %collective-permute-done.10), kind=kOutput, calls=%fused_computation.15 | convolution fusion | flops 37580963840 | bytes 54001664 | tf_op jit(solution)/shard_map/dot_general | solution.py:19
  415.9 146.0 %collective-permute-done = bf16[3584,2560]{1,0:T(8,128)(2,1)} collective-permute-done((bf16[3584,2560]{1,0:T(8,128)(2,1)}, bf16[3584,2560]{1,0:T(8,128)(2,1)}, u32[]{:S(2)}, u32[]{:S(2)}) %collective-permute-start) | collective-permute-done | bytes 18350112 | tf_op jit(solution)/shard_map/ppermute | solution.py:16
  580.0 60.6 %collective-permute-done.22 = bf16[512,3584]{1,0:T(8,128)(2,1)} collective-permute-done((bf16[512,3584]{1,0:T(8,128)(2,1)}, bf16[512,3584]{1,0:T(8,128)(2,1)}, u32[]{:S(2)}, u32[]{:S(2)}) %collective-permute-start.22) | collective-permute-done | bytes 3670048 | tf_op jit(solution)/shard_map/ppermute | solution.py:16
  657.0 62.2 %collective-permute-done.15 = bf16[512,3584]{1,0:T(8,128)(2,1)} collective-permute-done((bf16[512,3584]{1,0:T(8,128)(2,1)}, bf16[512,3584]{1,0:T(8,128)(2,1)}, u32[]{:S(2)}, u32[]{:S(2)}) %collective-permute-start.15) | collective-permute-done | bytes 3670048 | tf_op jit(solution)/shard_map/ppermute | solution.py:16
  753.9 47.6 %convolution_bitcast_fusion.1 = f32[2048,2560]{0,1:T(8,128)} fusion(bf16[3584,2560]{1,0:T(8,128)(2,1)} %collective-permute-done.4, bf16[2048,3584]{1,0:T(8,128)(2,1)} %collective-permute-done.10), kind=kOutput, calls=%fused_computation.14 | convolution fusion | flops 37580963840 | bytes 54001664 | tf_op jit(solution)/shard_map/dot_general | solution.py:19
  817.0 294.0 %collective-permute-done.2 = bf16[3584,2560]{1,0:T(8,128)(2,1)} collective-permute-done((bf16[3584,2560]{1,0:T(8,128)(2,1)}, bf16[3584,2560]{1,0:T(8,128)(2,1)}, u32[]{:S(2)}, u32[]{:S(2)}) %collective-permute-start.2) | collective-permute-done | bytes 18350112 | tf_op jit(solution)/shard_map/ppermute | solution.py:16
  1147.2 44.0 %collective-permute-done.18 = bf16[512,3584]{1,0:T(8,128)(2,1)} collective-permute-done((bf16[512,3584]{1,0:T(8,128)(2,1)}, bf16[512,3584]{1,0:T(8,128)(2,1)}, u32[]{:S(2)}, u32[]{:S(2)}) %collective-permute-start.18) | collective-permute-done | bytes 3670048 | tf_op jit(solution)/shard_map/ppermute | solution.py:16
  1351.0 47.4 %convolution_bitcast_fusion.5 = f32[2048,2560]{0,1:T(8,128)} fusion(bf16[3584,2560]{1,0:T(8,128)(2,1)} %collective-permute-done.4, bf16[2048,3584]{1,0:T(8,128)(2,1)} %param.4), kind=kOutput, calls=%fused_computation.18 | convolution fusion | flops 37580963840 | bytes 54001664 | tf_op jit(solution)/shard_map/dot_general | solution.py:19
  1399.9 47.4 %convolution_bitcast_fusion = f32[2048,2560]{0,1:T(8,128)} fusion(bf16[3584,2560]{1,0:T(8,128)(2,1)} %collective-permute-done.6, bf16[2048,3584]{1,0:T(8,128)(2,1)} %collective-permute-done.10), kind=kOutput, calls=%fused_computation.13 | convolution fusion | flops 37580963840 | bytes 54001664 | tf_op jit(solution)/shard_map/dot_general | solution.py:19
  1447.3 47.5 %convolution_bitcast_fusion.4 = f32[2048,2560]{0,1:T(8,128)} fusion(bf16[3584,2560]{1,0:T(8,128)(2,1)} %collective-permute-done.6, bf16[2048,3584]{1,0:T(8,128)(2,1)} %param.4), kind=kOutput, calls=%fused_computation.17 | convolution fusion | flops 37580963840 | bytes 54001664 | tf_op jit(solution)/shard_map/dot_general | solution.py:19
  1530.6 71.3 %maximum_select_fusion = bf16[2,2,2560,3584]{3,2,1,0:T(8,128)(2,1)} fusion(bf16[2,2,2560,1792]{3,2,1,0:T(8,128)(2,1)} %bitcast.9, bf16[2,2,2560,1792]{3,2,1,0:T(8,128)(2,1)} %bitcast.139, pred[]{:T(512)S(6)} %eq.11), kind=kLoop, calls=%fused_computation.2 | loop fusion | flops 330301440 | bytes 146800640 | tf_op jit(solution)/shard_map/jit(_where)/select_n | solution.py:47
  1601.8 71.8 %reverse_select_fusion.1 = bf16[2,2,2560,3584]{3,2,1,0:T(8,128)(2,1)} fusion(bf16[2,2,2560,3584]{3,2,1,0:T(8,128)(2,1)} %maximum_select_fusion, pred[]{:T(512)S(6)} %eq.10), kind=kLoop, calls=%fused_computation.1 | loop fusion | flops 36700160 | bytes 146800640 | tf_op jit(solution)/shard_map/jit(_where)/select_n | solution.py:50
  1673.6 71.9 %reverse_select_fusion = bf16[2,2,2560,3584]{3,2,1,0:T(8,128)(2,1)} fusion(bf16[2,2,2560,3584]{3,2,1,0:T(8,128)(2,1)} %reverse_select_fusion.1, pred[]{:T(512)S(6)} %eq.9), kind=kLoop, calls=%fused_computation | loop fusion | flops 36700160 | bytes 146800640 | tf_op jit(solution)/shard_map/jit(_where)/select_n | solution.py:51
  2025.4 58.0 %fusion.58 = f32[512,3584]{1,0:T(8,128)} fusion(bf16[10240,3584]{1,0:T(8,128)(2,1)} %bitcast.10, bf16[512,2560]{0,1:T(8,128)(2,1)} %collective-permute-done.34, bf16[512,2560]{0,1:T(8,128)(2,1)} %fusion.182, bf16[512,2560]{0,1:T(8,128)(2,1)} %collective-permute-done.33, bf16[512,2560]{0,1:T(8,128)(2,1)} %fusion.183), kind=kOutput, calls=%fused_computation.69 | convolution fusion | flops 37622906880 | bytes 91226112 | tf_op jit(solution)/shard_map/dot_general | solution.py:19
  2084.9 54.7 %collective-permute-done.13 = bf16[512,2560]{0,1:T(8,128)(2,1)} collective-permute-done((bf16[512,2560]{0,1:T(8,128)(2,1)}, bf16[512,2560]{0,1:T(8,128)(2,1)}, u32[]{:S(2)}, u32[]{:S(2)}) %collective-permute-start.13) | collective-permute-done | bytes 2621472 | tf_op jit(solution)/shard_map/ppermute | solution.py:16
  2141.1 58.2 %fusion.18 = f32[512,3584]{1,0:T(8,128)} fusion(bf16[10240,3584]{1,0:T(8,128)(2,1)} %bitcast.10, bf16[512,2560]{0,1:T(8,128)(2,1)} %collective-permute-done.13, bf16[512,2560]{0,1:T(8,128)(2,1)} %fusion.194, bf16[512,2560]{0,1:T(8,128)(2,1)} %collective-permute-done.12, bf16[512,2560]{0,1:T(8,128)(2,1)} %fusion.195), kind=kOutput, calls=%fused_computation.29 | convolution fusion | flops 37622906880 | bytes 91226112 | tf_op jit(solution)/shard_map/dot_general | solution.py:19
  2199.8 52.1 %collective-permute-done.20 = bf16[512,2560]{0,1:T(8,128)(2,1)} collective-permute-done((bf16[512,2560]{0,1:T(8,128)(2,1)}, bf16[512,2560]{0,1:T(8,128)(2,1)}, u32[]{:S(2)}, u32[]{:S(2)}) %collective-permute-start.20) | collective-permute-done | bytes 2621472 | tf_op jit(solution)/shard_map/ppermute | solution.py:16
  2252.5 58.1 %fusion.34 = f32[512,3584]{1,0:T(8,128)} fusion(bf16[10240,3584]{1,0:T(8,128)(2,1)} %bitcast.10, bf16[512,2560]{0,1:T(8,128)(2,1)} %collective-permute-done.20, bf16[512,2560]{0,1:T(8,128)(2,1)} %fusion.190, bf16[512,2560]{0,1:T(8,128)(2,1)} %collective-permute-done.19, bf16[512,2560]{0,1:T(8,128)(2,1)} %fusion.191), kind=kOutput, calls=%fused_computation.45 | convolution fusion | flops 37622906880 | bytes 91226112 | tf_op jit(solution)/shard_map/dot_general | solution.py:19
  2313.6 59.5 %fusion.50 = f32[512,3584]{1,0:T(8,128)} fusion(bf16[10240,3584]{1,0:T(8,128)(2,1)} %bitcast.10, bf16[512,2560]{0,1:T(8,128)(2,1)} %collective-permute-done.27, bf16[512,2560]{0,1:T(8,128)(2,1)} %fusion.186, bf16[512,2560]{0,1:T(8,128)(2,1)} %collective-permute-done.26, bf16[512,2560]{0,1:T(8,128)(2,1)S(1)} %copy-done.4), kind=kOutput, calls=%fused_computation.61 | convolution fusion | flops 37622906880 | bytes 91226112 | tf_op jit(solution)/shard_map/dot_general | solution.py:19
  2375.1 38.0 %collective-permute-done.14 = f32[512,3584]{1,0:T(8,128)} collective-permute-done((f32[512,3584]{1,0:T(8,128)}, f32[512,3584]{1,0:T(8,128)}, u32[]{:S(2)}, u32[]{:S(2)}) %collective-permute-start.14) | collective-permute-done | bytes 7340064 | tf_op jit(solution)/shard_map/ppermute | solution.py:16
  2413.7 61.4 %add_convert_fusion.2 = bf16[512,3584]{1,0:T(8,128)(2,1)} fusion(f32[512,3584]{1,0:T(8,128)} %collective-permute-done.14, bf16[10240,3584]{1,0:T(8,128)(2,1)} %bitcast.10, bf16[512,2560]{0,1:T(8,128)(2,1)} %collective-permute-done.8, bf16[512,2560]{0,1:T(8,128)(2,1)} %fusion.196, bf16[512,2560]{0,1:T(8,128)(2,1)} %collective-permute-done.3, ...), kind=kOutput, calls=%fused_computation.80 | convolution fusion | flops 37626576896 | bytes 94896128 | tf_op jit(solution)/shard_map/dot_general | solution.py:19
  2489.8 80.6 %collective-permute-done.21 = f32[512,3584]{1,0:T(8,128)} collective-permute-done((f32[512,3584]{1,0:T(8,128)}, f32[512,3584]{1,0:T(8,128)}, u32[]{:S(2)}, u32[]{:S(2)}) %collective-permute-start.21) | collective-permute-done | bytes 7340064 | tf_op jit(solution)/shard_map/ppermute | solution.py:16
  2571.0 61.4 %fusion.74 = bf16[2048,3584]{1,0:T(8,128)(2,1)} fusion(bf16[2048,3584]{1,0:T(8,128)(2,1)} %dynamic_update_slice.15, f32[512,3584]{1,0:T(8,128)} %collective-permute-done.21, bf16[10240,3584]{1,0:T(8,128)(2,1)} %bitcast.10, bf16[512,2560]{0,1:T(8,128)(2,1)} %collective-permute-done.17, bf16[512,2560]{0,1:T(8,128)(2,1)} %fusion.192, ...), kind=kOutput, calls=%fused_computation.113 | convolution fusion | flops 37626576896 | bytes 94896128 | tf_op jit(solution)/shard_map/dot_general | solution.py:19
  2634.5 93.3 %collective-permute-done.28 = f32[512,3584]{1,0:T(8,128)} collective-permute-done((f32[512,3584]{1,0:T(8,128)}, f32[512,3584]{1,0:T(8,128)}, u32[]{:S(2)}, u32[]{:S(2)}) %collective-permute-start.28) | collective-permute-done | bytes 7340064 | tf_op jit(solution)/shard_map/ppermute | solution.py:16
  2727.7 61.5 %fusion.77 = bf16[2048,3584]{1,0:T(8,128)(2,1)} fusion(bf16[2048,3584]{1,0:T(8,128)(2,1)} %fusion.74, f32[512,3584]{1,0:T(8,128)} %collective-permute-done.28, bf16[10240,3584]{1,0:T(8,128)(2,1)} %bitcast.10, bf16[512,2560]{0,1:T(8,128)(2,1)} %collective-permute-done.24, bf16[512,2560]{0,1:T(8,128)(2,1)} %fusion.188, ...), kind=kOutput, calls=%fused_computation.114 | convolution fusion | flops 37626576896 | bytes 94896128 | tf_op jit(solution)/shard_map/dot_general | solution.py:19
  2789.2 90.9 %collective-permute-done.35 = f32[512,3584]{1,0:T(8,128)} collective-permute-done((f32[512,3584]{1,0:T(8,128)}, f32[512,3584]{1,0:T(8,128)}, u32[]{:S(2)}, u32[]{:S(2)}) %collective-permute-start.35) | collective-permute-done | bytes 7340064 | tf_op jit(solution)/shard_map/ppermute | solution.py:16
  (117 shorter events, 694.2 us)
Async XLA Ops:
  0.0 318.9 %collective-permute-start.10 = (bf16[2048,3584]{1,0:T(8,128)(2,1)}, bf16[2048,3584]{1,0:T(8,128)(2,1)}, u32[]{:S(2)}, u32[]{:S(2)}) collective-permute-start(bf16[2048,3584]{1,0:T(8,128)(2,1)} %param.4), channel_id=1, source_target_pairs={{0,4},{4,0},{1,5},{5,1},{2,6},{6,2},{3,7},{7,3}} | collective-permute-start | bytes 44040200 | tf_op jit(solution)/shard_map/ppermute | solution.py:16
  7.5 744.3 %collective-permute-start.1 = (bf16[512,3584]{1,0:T(8,128)(2,1)}, bf16[512,3584]{1,0:T(8,128)(2,1)}, u32[]{:S(2)}, u32[]{:S(2)}) collective-permute-start(bf16[512,3584]{1,0:T(8,128)(2,1)} %slice.134), channel_id=1, source_target_pairs={{0,2},{2,0},{1,3},{3,1},{4,6},{6,4},{5,7},{7,5}} | collective-permute-start | bytes 11010056 | tf_op jit(solution)/shard_map/ppermute | solution.py:16
  16.8 398.7 %collective-permute-start.29 = (bf16[512,3584]{1,0:T(8,128)(2,1)}, bf16[512,3584]{1,0:T(8,128)(2,1)}, u32[]{:S(2)}, u32[]{:S(2)}) collective-permute-start(bf16[512,3584]{1,0:T(8,128)(2,1)} %get-tuple-element.11), channel_id=1, source_target_pairs={{0,2},{2,0},{1,3},{3,1},{4,6},{6,4},{5,7},{7,5}} | collective-permute-start | bytes 11010056 | tf_op jit(solution)/shard_map/ppermute | solution.py:16
  43.7 518.2 %collective-permute-start = (bf16[3584,2560]{1,0:T(8,128)(2,1)}, bf16[3584,2560]{1,0:T(8,128)(2,1)}, u32[]{:S(2)}, u32[]{:S(2)}) collective-permute-start(bf16[3584,2560]{1,0:T(8,128)(2,1)} %get-tuple-element.9), channel_id=1, source_target_pairs={{0,2},{2,0},{1,3},{3,1},{4,6},{6,4},{5,7},{7,5}} | collective-permute-start | bytes 55050248 | tf_op jit(solution)/shard_map/ppermute | solution.py:16
  45.2 706.7 %collective-permute-start.4 = (bf16[3584,2560]{1,0:T(8,128)(2,1)}, bf16[3584,2560]{1,0:T(8,128)(2,1)}, u32[]{:S(2)}, u32[]{:S(2)}) collective-permute-start(bf16[3584,2560]{1,0:T(8,128)(2,1)} %get-tuple-element.10), channel_id=1, source_target_pairs={{0,1},{1,0},{2,3},{3,2},{4,5},{5,4},{6,7},{7,6}} | collective-permute-start | bytes 55050248 | tf_op jit(solution)/shard_map/ppermute | solution.py:16
  318.9 321.6 %collective-permute-start.22 = (bf16[512,3584]{1,0:T(8,128)(2,1)}, bf16[512,3584]{1,0:T(8,128)(2,1)}, u32[]{:S(2)}, u32[]{:S(2)}) collective-permute-start(bf16[512,3584]{1,0:T(8,128)(2,1)} %get-tuple-element.12), channel_id=1, source_target_pairs={{0,2},{2,0},{1,3},{3,1},{4,6},{6,4},{5,7},{7,5}} | collective-permute-start | bytes 11010056 | tf_op jit(solution)/shard_map/ppermute | solution.py:16
  415.6 303.6 %collective-permute-start.15 = (bf16[512,3584]{1,0:T(8,128)(2,1)}, bf16[512,3584]{1,0:T(8,128)(2,1)}, u32[]{:S(2)}, u32[]{:S(2)}) collective-permute-start(bf16[512,3584]{1,0:T(8,128)(2,1)} %get-tuple-element.13), channel_id=1, source_target_pairs={{0,2},{2,0},{1,3},{3,1},{4,6},{6,4},{5,7},{7,5}} | collective-permute-start | bytes 11010056 | tf_op jit(solution)/shard_map/ppermute | solution.py:16
  561.9 549.1 %collective-permute-start.2 = (bf16[3584,2560]{1,0:T(8,128)(2,1)}, bf16[3584,2560]{1,0:T(8,128)(2,1)}, u32[]{:S(2)}, u32[]{:S(2)}) collective-permute-start(bf16[3584,2560]{1,0:T(8,128)(2,1)} %get-tuple-element.8), channel_id=1, source_target_pairs={{0,2},{2,0},{1,3},{3,1},{4,6},{6,4},{5,7},{7,5}} | collective-permute-start | bytes 55050248 | tf_op jit(solution)/shard_map/ppermute | solution.py:16
  719.2 679.2 %collective-permute-start.6 = (bf16[3584,2560]{1,0:T(8,128)(2,1)}, bf16[3584,2560]{1,0:T(8,128)(2,1)}, u32[]{:S(2)}, u32[]{:S(2)}) collective-permute-start(bf16[3584,2560]{1,0:T(8,128)(2,1)} %get-tuple-element.7), channel_id=1, source_target_pairs={{0,1},{1,0},{2,3},{3,2},{4,5},{5,4},{6,7},{7,6}} | collective-permute-start | bytes 55050248 | tf_op jit(solution)/shard_map/ppermute | solution.py:16
  735.9 794.1 %collective-permute-start.9 = (bf16[10240,1792]{1,0:T(8,128)(2,1)}, bf16[10240,1792]{1,0:T(8,128)(2,1)}, u32[]{:S(2)}, u32[]{:S(2)}) collective-permute-start(bf16[10240,1792]{1,0:T(8,128)(2,1)} %param.7), channel_id=1, source_target_pairs={{0,1},{1,0},{2,3},{3,2},{4,5},{5,4},{6,7},{7,6}} | collective-permute-start | bytes 110100488 | tf_op jit(solution)/shard_map/ppermute | solution.py:16
  751.8 377.1 %collective-permute-start.25 = (bf16[512,3584]{1,0:T(8,128)(2,1)}, bf16[512,3584]{1,0:T(8,128)(2,1)}, u32[]{:S(2)}, u32[]{:S(2)}) collective-permute-start(bf16[512,3584]{1,0:T(8,128)(2,1)} %collective-permute-done.22), channel_id=1, source_target_pairs={{0,4},{4,0},{1,5},{5,1},{2,6},{6,2},{3,7},{7,3}} | collective-permute-start | bytes 11010056 | tf_op jit(solution)/shard_map/ppermute | solution.py:16
  751.9 565.0 %collective-permute-start.11 = (bf16[512,3584]{1,0:T(8,128)(2,1)}, bf16[512,3584]{1,0:T(8,128)(2,1)}, u32[]{:S(2)}, u32[]{:S(2)}) collective-permute-start(bf16[512,3584]{1,0:T(8,128)(2,1)} %collective-permute-done.1), channel_id=1, source_target_pairs={{0,4},{4,0},{1,5},{5,1},{2,6},{6,2},{3,7},{7,3}} | collective-permute-start | bytes 11010056 | tf_op jit(solution)/shard_map/ppermute | solution.py:16
  1128.9 1244.2 %collective-permute-start.3 = (bf16[512,2560]{0,1:T(8,128)(2,1)}, bf16[512,2560]{0,1:T(8,128)(2,1)}, u32[]{:S(2)}, u32[]{:S(2)}) collective-permute-start(bf16[512,2560]{0,1:T(8,128)(2,1)} %fusion.197), channel_id=1, source_target_pairs={{0,2},{2,0},{1,3},{3,1},{4,6},{6,4},{5,7},{7,5}} | collective-permute-start | bytes 7864328 | tf_op jit(solution)/shard_map/ppermute | solution.py:16
  1191.3 303.5 %collective-permute-start.5 = (bf16[3584,2560]{1,0:T(8,128)(2,1)}, bf16[3584,2560]{1,0:T(8,128)(2,1)}, u32[]{:S(2)}, u32[]{:S(2)}) collective-permute-start(bf16[3584,2560]{1,0:T(8,128)(2,1)} %collective-permute-done), channel_id=1, source_target_pairs={{0,1},{1,0},{2,3},{3,2},{4,5},{5,4},{6,7},{7,6}} | collective-permute-start | bytes 55050248 | tf_op jit(solution)/shard_map/ppermute | solution.py:16
  1316.9 194.0 %collective-permute-start.7 = (bf16[3584,2560]{1,0:T(8,128)(2,1)}, bf16[3584,2560]{1,0:T(8,128)(2,1)}, u32[]{:S(2)}, u32[]{:S(2)}) collective-permute-start(bf16[3584,2560]{1,0:T(8,128)(2,1)} %collective-permute-done.2), channel_id=1, source_target_pairs={{0,1},{1,0},{2,3},{3,2},{4,5},{5,4},{6,7},{7,6}} | collective-permute-start | bytes 55050248 | tf_op jit(solution)/shard_map/ppermute | solution.py:16
  1398.4 1390.8 %collective-permute-start.31 = (bf16[512,2560]{0,1:T(8,128)(2,1)}, bf16[512,2560]{0,1:T(8,128)(2,1)}, u32[]{:S(2)}, u32[]{:S(2)}) collective-permute-start(bf16[512,2560]{0,1:T(8,128)(2,1)} %fusion.184), channel_id=1, source_target_pairs={{0,2},{2,0},{1,3},{3,1},{4,6},{6,4},{5,7},{7,5}} | collective-permute-start | bytes 7864328 | tf_op jit(solution)/shard_map/ppermute | solution.py:16
  1494.8 588.7 %collective-permute-start.12 = (bf16[512,2560]{0,1:T(8,128)(2,1)}, bf16[512,2560]{0,1:T(8,128)(2,1)}, u32[]{:S(2)}, u32[]{:S(2)}) collective-permute-start(bf16[512,2560]{0,1:T(8,128)(2,1)} %fusion.195), channel_id=1, source_target_pairs={{0,2},{2,0},{1,3},{3,1},{4,6},{6,4},{5,7},{7,5}} | collective-permute-start | bytes 7864328 | tf_op jit(solution)/shard_map/ppermute | solution.py:16
  1510.9 512.5 %collective-permute-start.33 = (bf16[512,2560]{0,1:T(8,128)(2,1)}, bf16[512,2560]{0,1:T(8,128)(2,1)}, u32[]{:S(2)}, u32[]{:S(2)}) collective-permute-start(bf16[512,2560]{0,1:T(8,128)(2,1)} %fusion.183), channel_id=1, source_target_pairs={{0,2},{2,0},{1,3},{3,1},{4,6},{6,4},{5,7},{7,5}} | collective-permute-start | bytes 7864328 | tf_op jit(solution)/shard_map/ppermute | solution.py:16
  1530.0 494.9 %collective-permute-start.34 = (bf16[512,2560]{0,1:T(8,128)(2,1)}, bf16[512,2560]{0,1:T(8,128)(2,1)}, u32[]{:S(2)}, u32[]{:S(2)}) collective-permute-start(bf16[512,2560]{0,1:T(8,128)(2,1)} %fusion.182), channel_id=1, source_target_pairs={{0,2},{2,0},{1,3},{3,1},{4,6},{6,4},{5,7},{7,5}} | collective-permute-start | bytes 7864328 | tf_op jit(solution)/shard_map/ppermute | solution.py:16
  2023.4 175.9 %collective-permute-start.19 = (bf16[512,2560]{0,1:T(8,128)(2,1)}, bf16[512,2560]{0,1:T(8,128)(2,1)}, u32[]{:S(2)}, u32[]{:S(2)}) collective-permute-start(bf16[512,2560]{0,1:T(8,128)(2,1)} %fusion.191), channel_id=1, source_target_pairs={{0,2},{2,0},{1,3},{3,1},{4,6},{6,4},{5,7},{7,5}} | collective-permute-start | bytes 7864328 | tf_op jit(solution)/shard_map/ppermute | solution.py:16
  2024.9 114.7 %collective-permute-start.13 = (bf16[512,2560]{0,1:T(8,128)(2,1)}, bf16[512,2560]{0,1:T(8,128)(2,1)}, u32[]{:S(2)}, u32[]{:S(2)}) collective-permute-start(bf16[512,2560]{0,1:T(8,128)(2,1)} %fusion.194), channel_id=1, source_target_pairs={{0,2},{2,0},{1,3},{3,1},{4,6},{6,4},{5,7},{7,5}} | collective-permute-start | bytes 7864328 | tf_op jit(solution)/shard_map/ppermute | solution.py:16
  2083.4 227.2 %collective-permute-start.26 = (bf16[512,2560]{0,1:T(8,128)(2,1)S(1)}, bf16[512,2560]{0,1:T(8,128)(2,1)}, u32[]{:S(2)}, u32[]{:S(2)}) collective-permute-start(bf16[512,2560]{0,1:T(8,128)(2,1)S(1)} %copy-done.4), channel_id=1, source_target_pairs={{0,2},{2,0},{1,3},{3,1},{4,6},{6,4},{5,7},{7,5}} | collective-permute-start | bytes 7864328 | tf_op jit(solution)/shard_map/ppermute | solution.py:16
  2199.3 112.8 %collective-permute-start.27 = (bf16[512,2560]{0,1:T(8,128)(2,1)}, bf16[512,2560]{0,1:T(8,128)(2,1)}, u32[]{:S(2)}, u32[]{:S(2)}) collective-permute-start(bf16[512,2560]{0,1:T(8,128)(2,1)} %fusion.186), channel_id=1, source_target_pairs={{0,2},{2,0},{1,3},{3,1},{4,6},{6,4},{5,7},{7,5}} | collective-permute-start | bytes 7864328 | tf_op jit(solution)/shard_map/ppermute | solution.py:16
  2252.0 161.2 %collective-permute-start.14 = (f32[512,3584]{1,0:T(8,128)}, f32[512,3584]{1,0:T(8,128)}, u32[]{:S(2)}, u32[]{:S(2)}) collective-permute-start(f32[512,3584]{1,0:T(8,128)} %fusion.18), channel_id=1, source_target_pairs={{0,4},{4,0},{1,5},{5,1},{2,6},{6,2},{3,7},{7,3}} | collective-permute-start | bytes 22020104 | tf_op jit(solution)/shard_map/ppermute | solution.py:16
  2312.1 258.4 %collective-permute-start.21 = (f32[512,3584]{1,0:T(8,128)}, f32[512,3584]{1,0:T(8,128)}, u32[]{:S(2)}, u32[]{:S(2)}) collective-permute-start(f32[512,3584]{1,0:T(8,128)} %fusion.34), channel_id=1, source_target_pairs={{0,4},{4,0},{1,5},{5,1},{2,6},{6,2},{3,7},{7,3}} | collective-permute-start | bytes 22020104 | tf_op jit(solution)/shard_map/ppermute | solution.py:16
  2373.6 115.7 %collective-permute-start.17 = (bf16[512,2560]{0,1:T(8,128)(2,1)}, bf16[512,2560]{0,1:T(8,128)(2,1)}, u32[]{:S(2)}, u32[]{:S(2)}) collective-permute-start(bf16[512,2560]{0,1:T(8,128)(2,1)} %fusion.192), channel_id=1, source_target_pairs={{0,2},{2,0},{1,3},{3,1},{4,6},{6,4},{5,7},{7,5}} | collective-permute-start | bytes 7864328 | tf_op jit(solution)/shard_map/ppermute | solution.py:16
  2413.1 314.6 %collective-permute-start.28 = (f32[512,3584]{1,0:T(8,128)}, f32[512,3584]{1,0:T(8,128)}, u32[]{:S(2)}, u32[]{:S(2)}) collective-permute-start(f32[512,3584]{1,0:T(8,128)} %fusion.50), channel_id=1, source_target_pairs={{0,4},{4,0},{1,5},{5,1},{2,6},{6,2},{3,7},{7,3}} | collective-permute-start | bytes 22020104 | tf_op jit(solution)/shard_map/ppermute | solution.py:16
  2481.7 150.8 %collective-permute-start.23 = (bf16[512,2560]{0,1:T(8,128)(2,1)}, bf16[512,2560]{0,1:T(8,128)(2,1)}, u32[]{:S(2)}, u32[]{:S(2)}) collective-permute-start(bf16[512,2560]{0,1:T(8,128)(2,1)} %fusion.189), channel_id=1, source_target_pairs={{0,2},{2,0},{1,3},{3,1},{4,6},{6,4},{5,7},{7,5}} | collective-permute-start | bytes 7864328 | tf_op jit(solution)/shard_map/ppermute | solution.py:16
  2489.3 144.6 %collective-permute-start.24 = (bf16[512,2560]{0,1:T(8,128)(2,1)}, bf16[512,2560]{0,1:T(8,128)(2,1)}, u32[]{:S(2)}, u32[]{:S(2)}) collective-permute-start(bf16[512,2560]{0,1:T(8,128)(2,1)} %fusion.188), channel_id=1, source_target_pairs={{0,2},{2,0},{1,3},{3,1},{4,6},{6,4},{5,7},{7,5}} | collective-permute-start | bytes 7864328 | tf_op jit(solution)/shard_map/ppermute | solution.py:16
  2570.4 309.6 %collective-permute-start.35 = (f32[512,3584]{1,0:T(8,128)}, f32[512,3584]{1,0:T(8,128)}, u32[]{:S(2)}, u32[]{:S(2)}) collective-permute-start(f32[512,3584]{1,0:T(8,128)} %fusion.58), channel_id=1, source_target_pairs={{0,4},{4,0},{1,5},{5,1},{2,6},{6,2},{3,7},{7,3}} | collective-permute-start | bytes 22020104 | tf_op jit(solution)/shard_map/ppermute | solution.py:16
  2632.4 283.1 %collective-permute-start.36 = (bf16[256,2560]{0,1:T(8,128)(2,1)S(1)}, bf16[256,2560]{0,1:T(8,128)(2,1)}, u32[]{:S(2)}, u32[]{:S(2)}) collective-permute-start(bf16[256,2560]{0,1:T(8,128)(2,1)S(1)} %copy-done.3), channel_id=1, source_target_pairs={{0,2},{2,0},{1,3},{3,1},{4,6},{6,4},{5,7},{7,5}} | collective-permute-start | bytes 3932168 | tf_op jit(solution)/shard_map/ppermute | solution.py:16
  2633.9 267.7 %collective-permute-start.30 = (bf16[256,2560]{0,1:T(8,128)(2,1)}, bf16[256,2560]{0,1:T(8,128)(2,1)}, u32[]{:S(2)}, u32[]{:S(2)}) collective-permute-start(bf16[256,2560]{0,1:T(8,128)(2,1)} %get-tuple-element.15), channel_id=1, source_target_pairs={{0,2},{2,0},{1,3},{3,1},{4,6},{6,4},{5,7},{7,5}} | collective-permute-start | bytes 3932168 | tf_op jit(solution)/shard_map/ppermute | solution.py:16
  (12 other events, 757.0 us)

commit v3 on v2

--- a/solution.py
+++ b/solution.py
@@ -62,6 +62,9 @@
             r = (i % CHUNKS) * rows
             return parts[w, "o" if i < CHUNKS else "m", j][r:r + rows]
 
+        half_c, half_r = cols // 2, rows // 2
+        tail = [(0, rows, 0, half_c), (0, rows, half_c, half_c + half_c // 2)]
+        tail += [(k * half_r, (k + 1) * half_r, half_c + half_c // 2, cols) for k in range(2)]
         gates, hidden, hidden_far = {}, {}, {}
         for i in range(n):
             for j in range(2):
@@ -70,8 +73,8 @@
                 gate = gates[i, j].astype(jnp.float32)
                 hidden[i, j] = (jax.nn.silu(gate) * up).astype(jnp.bfloat16)
                 if (i, j) == (n - 1, 1):
-                    hidden_far[i, j] = [swap(hidden[i, j][k * rows // 2:(k + 1) * rows // 2], "dy")
-                                        for k in range(2)]
+                    hidden_far[i, j] = [swap(hidden[i, j][r0:r1, c0:c1], "dy")
+                                        for r0, r1, c0, c1 in tail]
                 else:
                     hidden_far[i, j] = swap(hidden[i, j], "dy")
 
@@ -88,12 +91,16 @@
                 out = lax.dynamic_update_slice(out, z_part, ((i - CHUNKS) * rows, 0))
         i = n - 1
         z_part = dot(hidden[i, 1], wd_perm[2 * cols:3 * cols]) + z_from[CHUNKS - 1]
-        z_part = dot(hidden[i, 0], wd_perm[:cols]) + z_part
-        z_part = dot(hidden_far[i, 0], wd_perm[cols:2 * cols]) + z_part
-        for k in range(2):
-            z_half = dot(hidden_far[i, 1][k], wd_perm[3 * cols:]) + z_part[k * rows // 2:(k + 1) * rows // 2]
-            z_half = z_half.astype(jnp.bfloat16)
-            out = lax.dynamic_update_slice(out, z_half, ((CHUNKS - 1) * rows + k * rows // 2, 0))
+        z_part = lax.optimization_barrier(dot(hidden[i, 0], wd_perm[:cols]) + z_part)
+        z_part = lax.optimization_barrier(dot(hidden_far[i, 0], wd_perm[cols:2 * cols]) + z_part)
+        for k, (r0, r1, c0, c1) in enumerate(tail):
+            z_piece = dot(hidden_far[i, 1][k], wd_perm[3 * cols + c0:3 * cols + c1]) + z_part[r0:r1]
+            if c1 == cols:
+                z_piece = z_piece.astype(jnp.bfloat16)
+            if c1 == cols:
+                out = lax.dynamic_update_slice(out, z_piece, ((CHUNKS - 1) * rows + r0, 0))
+            else:
+                z_part = z_piece
         return out
 
     return jax.shard_map(body, mesh=mesh, in_specs=(x_spec, w_in_spec, w_in_spec, w_out_spec),

time: 2940 us -> 2990 us (1.017)
  waiting for transfers between devices: 1180 us -> 1210 us
    ppermute x37 -> x39, waiting for transfers between devices: 1180 us -> 1210 us  [swap(): return lax.ppermute(arr, axis, [(0, 1), (1, 0)])]
    dot_general x52 -> x54, matrix products: 1430 us -> 1430 us  [dot(): return jnp.dot(lhs, rhs, preferred_element_type=jnp.float32)]
  transfers between devices with their start and end apart: 37 -> 39, of which waited for: 13 -> 12; matrix products, arithmetic and copies ran while one was open for 58% -> 58% of each run, Pallas kernels for 0% -> 0%
where the time goes in v3:
time: 2990 us; the launch traced here: 2980 us
  matrix products  1430 us (48%)
  waiting for transfers between devices  1210 us (40%)
  other arithmetic  227 us (8%)
  local copies, waits for them, and re-layouts  74.3 us (2%)
  starting transfers between devices  35.1 us (1%)
    dot_general x54, matrix products, dot(): return jnp.dot(lhs, rhs, preferred_element_type=jnp.float32)  1430 us
    ppermute x39, waiting for transfers between devices, swap(): return lax.ppermute(arr, axis, [(0, 1), (1, 0)])  1210 us
    select_n x1, other arithmetic, body(): wd4 = jnp.where(my_y == 1, lax.rev(wd4, (1,)), wd4)  72 us
    select_n x1, other arithmetic, body(): wd4 = jnp.where(my_c == 1, lax.rev(wd4, (0,)), wd4)  71.7 us
    select_n x1, other arithmetic, body(): jnp.where(my_c == 0, jnp.concatenate([wd_blk, wd_other], axis=1), jnp.con...  71.2 us
  transfers between devices with their start and end apart: 39, of which 12 were waited for; matrix products, arithmetic and copies ran while one was open for 58% of the time, Pallas kernels for 0%

profile of v3, /device:TPU:0, one launch (start us, length us, event | category | flops | bytes accessed | tf_op | source)
XLA Modules:
  0.0 2979.6 jit_solution(1536744310153187357)
XLA Ops:
  17.3 26.3 constant_dynamic-slice_fusion.2
  45.2 26.3 constant_dynamic-slice_fusion.1
  71.5 47.1 %convolution_bitcast_fusion.7 = f32[2048,2560]{0,1:T(8,128)} fusion(bf16[3584,2560]{1,0:T(8,128)(2,1)} %get-tuple-element.10, bf16[2048,3584]{1,0:T(8,128)(2,1)} %param.4), kind=kOutput, calls=%fused_computation.16 | convolution fusion | flops 37580963840 | bytes 54001664 | tf_op jit(solution)/shard_map/dot_general | solution.py:19
  118.7 47.4 %convolution_bitcast_fusion.6 = f32[2048,2560]{0,1:T(8,128)} fusion(bf16[3584,2560]{1,0:T(8,128)(2,1)} %get-tuple-element.7, bf16[2048,3584]{1,0:T(8,128)(2,1)} %param.4), kind=kOutput, calls=%fused_computation.15 | convolution fusion | flops 37580963840 | bytes 54001664 | tf_op jit(solution)/shard_map/dot_general | solution.py:19
  166.0 152.9 %collective-permute-done.10 = bf16[2048,3584]{1,0:T(8,128)(2,1)} collective-permute-done((bf16[2048,3584]{1,0:T(8,128)(2,1)}, bf16[2048,3584]{1,0:T(8,128)(2,1)}, u32[]{:S(2)}, u32[]{:S(2)}) %collective-permute-start.10) | collective-permute-done | bytes 14680096 | tf_op jit(solution)/shard_map/ppermute | solution.py:16
  320.6 47.8 %convolution_bitcast_fusion.3 = f32[2048,2560]{0,1:T(8,128)} fusion(bf16[3584,2560]{1,0:T(8,128)(2,1)} %get-tuple-element.10, bf16[2048,3584]{1,0:T(8,128)(2,1)} %collective-permute-done.10), kind=kOutput, calls=%fused_computation.12 | convolution fusion | flops 37580963840 | bytes 54001664 | tf_op jit(solution)/shard_map/dot_general | solution.py:19
  368.5 47.3 %convolution_bitcast_fusion.2 = f32[2048,2560]{0,1:T(8,128)} fusion(bf16[3584,2560]{1,0:T(8,128)(2,1)} %get-tuple-element.7, bf16[2048,3584]{1,0:T(8,128)(2,1)} %collective-permute-done.10), kind=kOutput, calls=%fused_computation.11 | convolution fusion | flops 37580963840 | bytes 54001664 | tf_op jit(solution)/shard_map/dot_general | solution.py:19
  416.1 145.8 %collective-permute-done = bf16[3584,2560]{1,0:T(8,128)(2,1)} collective-permute-done((bf16[3584,2560]{1,0:T(8,128)(2,1)}, bf16[3584,2560]{1,0:T(8,128)(2,1)}, u32[]{:S(2)}, u32[]{:S(2)}) %collective-permute-start) | collective-permute-done | bytes 18350112 | tf_op jit(solution)/shard_map/ppermute | solution.py:16
  580.0 60.5 %collective-permute-done.22 = bf16[512,3584]{1,0:T(8,128)(2,1)} collective-permute-done((bf16[512,3584]{1,0:T(8,128)(2,1)}, bf16[512,3584]{1,0:T(8,128)(2,1)}, u32[]{:S(2)}, u32[]{:S(2)}) %collective-permute-start.22) | collective-permute-done | bytes 3670048 | tf_op jit(solution)/shard_map/ppermute | solution.py:16
  657.0 62.2 %collective-permute-done.15 = bf16[512,3584]{1,0:T(8,128)(2,1)} collective-permute-done((bf16[512,3584]{1,0:T(8,128)(2,1)}, bf16[512,3584]{1,0:T(8,128)(2,1)}, u32[]{:S(2)}, u32[]{:S(2)}) %collective-permute-start.15) | collective-permute-done | bytes 3670048 | tf_op jit(solution)/shard_map/ppermute | solution.py:16
  754.0 47.3 %convolution_bitcast_fusion.1 = f32[2048,2560]{0,1:T(8,128)} fusion(bf16[3584,2560]{1,0:T(8,128)(2,1)} %collective-permute-done.4, bf16[2048,3584]{1,0:T(8,128)(2,1)} %collective-permute-done.10), kind=kOutput, calls=%fused_computation.10 | convolution fusion | flops 37580963840 | bytes 54001664 | tf_op jit(solution)/shard_map/dot_general | solution.py:19
  816.9 294.1 %collective-permute-done.2 = bf16[3584,2560]{1,0:T(8,128)(2,1)} collective-permute-done((bf16[3584,2560]{1,0:T(8,128)(2,1)}, bf16[3584,2560]{1,0:T(8,128)(2,1)}, u32[]{:S(2)}, u32[]{:S(2)}) %collective-permute-start.2) | collective-permute-done | bytes 18350112 | tf_op jit(solution)/shard_map/ppermute | solution.py:16
  1147.6 43.7 %collective-permute-done.18 = bf16[512,3584]{1,0:T(8,128)(2,1)} collective-permute-done((bf16[512,3584]{1,0:T(8,128)(2,1)}, bf16[512,3584]{1,0:T(8,128)(2,1)}, u32[]{:S(2)}, u32[]{:S(2)}) %collective-permute-start.18) | collective-permute-done | bytes 3670048 | tf_op jit(solution)/shard_map/ppermute | solution.py:16
  1280.0 18.9 fusion.182
  1350.3 47.4 %convolution_bitcast_fusion.5 = f32[2048,2560]{0,1:T(8,128)} fusion(bf16[3584,2560]{1,0:T(8,128)(2,1)} %collective-permute-done.4, bf16[2048,3584]{1,0:T(8,128)(2,1)} %param.4), kind=kOutput, calls=%fused_computation.14 | convolution fusion | flops 37580963840 | bytes 54001664 | tf_op jit(solution)/shard_map/dot_general | solution.py:19
  1399.2 47.5 %convolution_bitcast_fusion = f32[2048,2560]{0,1:T(8,128)} fusion(bf16[3584,2560]{1,0:T(8,128)(2,1)} %collective-permute-done.6, bf16[2048,3584]{1,0:T(8,128)(2,1)} %collective-permute-done.10), kind=kOutput, calls=%fused_computation.9 | convolution fusion | flops 37580963840 | bytes 54001664 | tf_op jit(solution)/shard_map/dot_general | solution.py:19
  1446.7 47.4 %convolution_bitcast_fusion.4 = f32[2048,2560]{0,1:T(8,128)} fusion(bf16[3584,2560]{1,0:T(8,128)(2,1)} %collective-permute-done.6, bf16[2048,3584]{1,0:T(8,128)(2,1)} %param.4), kind=kOutput, calls=%fused_computation.13 | convolution fusion | flops 37580963840 | bytes 54001664 | tf_op jit(solution)/shard_map/dot_general | solution.py:19
  1569.0 71.2 %maximum_select_fusion = bf16[2,2,2560,3584]{3,2,1,0:T(8,128)(2,1)} fusion(bf16[2,2,2560,1792]{3,2,1,0:T(8,128)(2,1)} %bitcast.9, bf16[2,2,2560,1792]{3,2,1,0:T(8,128)(2,1)} %bitcast.141, pred[]{:T(512)S(6)} %eq.11), kind=kLoop, calls=%fused_computation.2 | loop fusion | flops 330301440 | bytes 146800640 | tf_op jit(solution)/shard_map/jit(_where)/select_n | solution.py:47
  1640.3 71.7 %reverse_select_fusion.1 = bf16[2,2,2560,3584]{3,2,1,0:T(8,128)(2,1)} fusion(bf16[2,2,2560,3584]{3,2,1,0:T(8,128)(2,1)} %maximum_select_fusion, pred[]{:T(512)S(6)} %eq.10), kind=kLoop, calls=%fused_computation.1 | loop fusion | flops 36700160 | bytes 146800640 | tf_op jit(solution)/shard_map/jit(_where)/select_n | solution.py:50
  1712.0 72.0 %reverse_select_fusion = bf16[2,2,2560,3584]{3,2,1,0:T(8,128)(2,1)} fusion(bf16[2,2,2560,3584]{3,2,1,0:T(8,128)(2,1)} %reverse_select_fusion.1, pred[]{:T(512)S(6)} %eq.9), kind=kLoop, calls=%fused_computation | loop fusion | flops 36700160 | bytes 146800640 | tf_op jit(solution)/shard_map/jit(_where)/select_n | solution.py:51
  2039.3 57.9 %fusion.54 = f32[512,3584]{1,0:T(8,128)} fusion(bf16[10240,3584]{1,0:T(8,128)(2,1)} %bitcast.10, bf16[512,2560]{0,1:T(8,128)(2,1)} %collective-permute-done.36, bf16[512,2560]{0,1:T(8,128)(2,1)} %fusion.175, bf16[512,2560]{0,1:T(8,128)(2,1)} %collective-permute-done.35, bf16[512,2560]{0,1:T(8,128)(2,1)} %fusion.176), kind=kOutput, calls=%fused_computation.65 | convolution fusion | flops 37622906880 | bytes 91226112 | tf_op jit(solution)/shard_map/dot_general | solution.py:19
  2097.9 98.2 %collective-permute-done.13 = bf16[512,2560]{0,1:T(8,128)(2,1)} collective-permute-done((bf16[512,2560]{0,1:T(8,128)(2,1)}, bf16[512,2560]{0,1:T(8,128)(2,1)}, u32[]{:S(2)}, u32[]{:S(2)}) %collective-permute-start.13) | collective-permute-done | bytes 2621472 | tf_op jit(solution)/shard_map/ppermute | solution.py:16
  2197.6 58.4 %fusion.14 = f32[512,3584]{1,0:T(8,128)} fusion(bf16[10240,3584]{1,0:T(8,128)(2,1)} %bitcast.10, bf16[512,2560]{0,1:T(8,128)(2,1)} %collective-permute-done.13, bf16[512,2560]{0,1:T(8,128)(2,1)} %fusion.187, bf16[512,2560]{0,1:T(8,128)(2,1)} %collective-permute-done.12, bf16[512,2560]{0,1:T(8,128)(2,1)} %fusion.188), kind=kOutput, calls=%fused_computation.25 | convolution fusion | flops 37622906880 | bytes 91226112 | tf_op jit(solution)/shard_map/dot_general | solution.py:19
  2258.0 58.1 %fusion.30 = f32[512,3584]{1,0:T(8,128)} fusion(bf16[10240,3584]{1,0:T(8,128)(2,1)} %bitcast.10, bf16[512,2560]{0,1:T(8,128)(2,1)} %collective-permute-done.20, bf16[512,2560]{0,1:T(8,128)(2,1)} %fusion.183, bf16[512,2560]{0,1:T(8,128)(2,1)} %collective-permute-done.19, bf16[512,2560]{0,1:T(8,128)(2,1)} %fusion.184), kind=kOutput, calls=%fused_computation.41 | convolution fusion | flops 37622906880 | bytes 91226112 | tf_op jit(solution)/shard_map/dot_general | solution.py:19
  2317.2 59.2 %fusion.46 = f32[512,3584]{1,0:T(8,128)} fusion(bf16[10240,3584]{1,0:T(8,128)(2,1)} %bitcast.10, bf16[512,2560]{0,1:T(8,128)(2,1)} %collective-permute-done.27, bf16[512,2560]{0,1:T(8,128)(2,1)} %fusion.179, bf16[512,2560]{0,1:T(8,128)(2,1)} %collective-permute-done.26, bf16[512,2560]{0,1:T(8,128)(2,1)S(1)} %copy-done.5), kind=kOutput, calls=%fused_computation.57 | convolution fusion | flops 37622906880 | bytes 91226112 | tf_op jit(solution)/shard_map/dot_general | solution.py:19
  2376.4 198.1 %collective-permute-done.37 = f32[512,3584]{1,0:T(8,128)} collective-permute-done((f32[512,3584]{1,0:T(8,128)}, f32[512,3584]{1,0:T(8,128)}, u32[]{:S(2)}, u32[]{:S(2)}) %collective-permute-start.37) | collective-permute-done | bytes 7340064 | tf_op jit(solution)/shard_map/ppermute | solution.py:16
  2590.1 62.7 %add_convert_fusion.2 = bf16[512,3584]{1,0:T(8,128)(2,1)} fusion(f32[512,3584]{1,0:T(8,128)} %collective-permute-done.14, bf16[10240,3584]{1,0:T(8,128)(2,1)} %bitcast.10, bf16[512,2560]{0,1:T(8,128)(2,1)} %collective-permute-done.8, bf16[512,2560]{0,1:T(8,128)(2,1)S(1)} %copy-done.6, bf16[512,2560]{0,1:T(8,128)(2,1)} %collective-permute-done.3, ...), kind=kOutput, calls=%fused_computation.79 | convolution fusion | flops 37626576896 | bytes 94896128 | tf_op jit(solution)/shard_map/dot_general | solution.py:19
  2659.4 31.3 %collective-permute-done.16 = bf16[512,2560]{0,1:T(8,128)(2,1)} collective-permute-done((bf16[512,2560]{0,1:T(8,128)(2,1)}, bf16[512,2560]{0,1:T(8,128)(2,1)}, u32[]{:S(2)}, u32[]{:S(2)}) %collective-permute-start.16) | collective-permute-done | bytes 2621472 | tf_op jit(solution)/shard_map/ppermute | solution.py:16
  2691.2 55.6 %collective-permute-done.17 = bf16[512,2560]{0,1:T(8,128)(2,1)} collective-permute-done((bf16[512,2560]{0,1:T(8,128)(2,1)}, bf16[512,2560]{0,1:T(8,128)(2,1)}, u32[]{:S(2)}, u32[]{:S(2)}) %collective-permute-start.17) | collective-permute-done | bytes 2621472 | tf_op jit(solution)/shard_map/ppermute | solution.py:16
  2748.9 61.4 %fusion.73 = bf16[2048,3584]{1,0:T(8,128)(2,1)} fusion(bf16[2048,3584]{1,0:T(8,128)(2,1)} %dynamic_update_slice.15, f32[512,3584]{1,0:T(8,128)} %collective-permute-done.21, bf16[10240,3584]{1,0:T(8,128)(2,1)} %bitcast.10, bf16[512,2560]{0,1:T(8,128)(2,1)} %collective-permute-done.17, bf16[512,2560]{0,1:T(8,128)(2,1)} %fusion.185, ...), kind=kOutput, calls=%fused_computation.113 | convolution fusion | flops 37626576896 | bytes 94896128 | tf_op jit(solution)/shard_map/dot_general | solution.py:19
  2810.8 54.6 %collective-permute-done.24 = bf16[512,2560]{0,1:T(8,128)(2,1)} collective-permute-done((bf16[512,2560]{0,1:T(8,128)(2,1)}, bf16[512,2560]{0,1:T(8,128)(2,1)}, u32[]{:S(2)}, u32[]{:S(2)}) %collective-permute-start.24) | collective-permute-done | bytes 2621472 | tf_op jit(solution)/shard_map/ppermute | solution.py:16
  2883.8 61.4 %fusion.76 = bf16[2048,3584]{1,0:T(8,128)(2,1)} fusion(bf16[2048,3584]{1,0:T(8,128)(2,1)} %fusion.73, f32[512,3584]{1,0:T(8,128)} %collective-permute-done.28, bf16[10240,3584]{1,0:T(8,128)(2,1)} %bitcast.10, bf16[512,2560]{0,1:T(8,128)(2,1)} %collective-permute-done.24, bf16[512,2560]{0,1:T(8,128)(2,1)} %fusion.181, ...), kind=kOutput, calls=%fused_computation.114 | convolution fusion | flops 37626576896 | bytes 94896128 | tf_op jit(solution)/shard_map/dot_general | solution.py:19
  (132 shorter events, 697.1 us)
Async XLA Ops:
  0.0 318.9 %collective-permute-start.10 = (bf16[2048,3584]{1,0:T(8,128)(2,1)}, bf16[2048,3584]{1,0:T(8,128)(2,1)}, u32[]{:S(2)}, u32[]{:S(2)}) collective-permute-start(bf16[2048,3584]{1,0:T(8,128)(2,1)} %param.4), channel_id=1, source_target_pairs={{0,4},{4,0},{1,5},{5,1},{2,6},{6,2},{3,7},{7,3}} | collective-permute-start | bytes 44040200 | tf_op jit(solution)/shard_map/ppermute | solution.py:16
  7.5 744.5 %collective-permute-start.1 = (bf16[512,3584]{1,0:T(8,128)(2,1)}, bf16[512,3584]{1,0:T(8,128)(2,1)}, u32[]{:S(2)}, u32[]{:S(2)}) collective-permute-start(bf16[512,3584]{1,0:T(8,128)(2,1)} %slice.146), channel_id=1, source_target_pairs={{0,2},{2,0},{1,3},{3,1},{4,6},{6,4},{5,7},{7,5}} | collective-permute-start | bytes 11010056 | tf_op jit(solution)/shard_map/ppermute | solution.py:16
  16.8 398.9 %collective-permute-start.29 = (bf16[512,3584]{1,0:T(8,128)(2,1)}, bf16[512,3584]{1,0:T(8,128)(2,1)}, u32[]{:S(2)}, u32[]{:S(2)}) collective-permute-start(bf16[512,3584]{1,0:T(8,128)(2,1)} %get-tuple-element.11), channel_id=1, source_target_pairs={{0,2},{2,0},{1,3},{3,1},{4,6},{6,4},{5,7},{7,5}} | collective-permute-start | bytes 11010056 | tf_op jit(solution)/shard_map/ppermute | solution.py:16
  43.7 518.2 %collective-permute-start = (bf16[3584,2560]{1,0:T(8,128)(2,1)}, bf16[3584,2560]{1,0:T(8,128)(2,1)}, u32[]{:S(2)}, u32[]{:S(2)}) collective-permute-start(bf16[3584,2560]{1,0:T(8,128)(2,1)} %get-tuple-element.9), channel_id=1, source_target_pairs={{0,2},{2,0},{1,3},{3,1},{4,6},{6,4},{5,7},{7,5}} | collective-permute-start | bytes 55050248 | tf_op jit(solution)/shard_map/ppermute | solution.py:16
  45.2 706.8 %collective-permute-start.4 = (bf16[3584,2560]{1,0:T(8,128)(2,1)}, bf16[3584,2560]{1,0:T(8,128)(2,1)}, u32[]{:S(2)}, u32[]{:S(2)}) collective-permute-start(bf16[3584,2560]{1,0:T(8,128)(2,1)} %get-tuple-element.10), channel_id=1, source_target_pairs={{0,1},{1,0},{2,3},{3,2},{4,5},{5,4},{6,7},{7,6}} | collective-permute-start | bytes 55050248 | tf_op jit(solution)/shard_map/ppermute | solution.py:16
  318.9 321.6 %collective-permute-start.22 = (bf16[512,3584]{1,0:T(8,128)(2,1)}, bf16[512,3584]{1,0:T(8,128)(2,1)}, u32[]{:S(2)}, u32[]{:S(2)}) collective-permute-start(bf16[512,3584]{1,0:T(8,128)(2,1)} %get-tuple-element.12), channel_id=1, source_target_pairs={{0,2},{2,0},{1,3},{3,1},{4,6},{6,4},{5,7},{7,5}} | collective-permute-start | bytes 11010056 | tf_op jit(solution)/shard_map/ppermute | solution.py:16
  415.8 303.4 %collective-permute-start.15 = (bf16[512,3584]{1,0:T(8,128)(2,1)}, bf16[512,3584]{1,0:T(8,128)(2,1)}, u32[]{:S(2)}, u32[]{:S(2)}) collective-permute-start(bf16[512,3584]{1,0:T(8,128)(2,1)} %get-tuple-element.13), channel_id=1, source_target_pairs={{0,2},{2,0},{1,3},{3,1},{4,6},{6,4},{5,7},{7,5}} | collective-permute-start | bytes 11010056 | tf_op jit(solution)/shard_map/ppermute | solution.py:16
  561.9 549.1 %collective-permute-start.2 = (bf16[3584,2560]{1,0:T(8,128)(2,1)}, bf16[3584,2560]{1,0:T(8,128)(2,1)}, u32[]{:S(2)}, u32[]{:S(2)}) collective-permute-start(bf16[3584,2560]{1,0:T(8,128)(2,1)} %get-tuple-element.8), channel_id=1, source_target_pairs={{0,2},{2,0},{1,3},{3,1},{4,6},{6,4},{5,7},{7,5}} | collective-permute-start | bytes 55050248 | tf_op jit(solution)/shard_map/ppermute | solution.py:16
  719.2 678.5 %collective-permute-start.6 = (bf16[3584,2560]{1,0:T(8,128)(2,1)}, bf16[3584,2560]{1,0:T(8,128)(2,1)}, u32[]{:S(2)}, u32[]{:S(2)}) collective-permute-start(bf16[3584,2560]{1,0:T(8,128)(2,1)} %get-tuple-element.7), channel_id=1, source_target_pairs={{0,1},{1,0},{2,3},{3,2},{4,5},{5,4},{6,7},{7,6}} | collective-permute-start | bytes 55050248 | tf_op jit(solution)/shard_map/ppermute | solution.py:16
  736.1 832.4 %collective-permute-start.9 = (bf16[10240,1792]{1,0:T(8,128)(2,1)}, bf16[10240,1792]{1,0:T(8,128)(2,1)}, u32[]{:S(2)}, u32[]{:S(2)}) collective-permute-start(bf16[10240,1792]{1,0:T(8,128)(2,1)} %param.7), channel_id=1, source_target_pairs={{0,1},{1,0},{2,3},{3,2},{4,5},{5,4},{6,7},{7,6}} | collective-permute-start | bytes 110100488 | tf_op jit(solution)/shard_map/ppermute | solution.py:16
  752.0 377.0 %collective-permute-start.25 = (bf16[512,3584]{1,0:T(8,128)(2,1)}, bf16[512,3584]{1,0:T(8,128)(2,1)}, u32[]{:S(2)}, u32[]{:S(2)}) collective-permute-start(bf16[512,3584]{1,0:T(8,128)(2,1)} %collective-permute-done.22), channel_id=1, source_target_pairs={{0,4},{4,0},{1,5},{5,1},{2,6},{6,2},{3,7},{7,3}} | collective-permute-start | bytes 11010056 | tf_op jit(solution)/shard_map/ppermute | solution.py:16
  752.0 564.5 %collective-permute-start.11 = (bf16[512,3584]{1,0:T(8,128)(2,1)}, bf16[512,3584]{1,0:T(8,128)(2,1)}, u32[]{:S(2)}, u32[]{:S(2)}) collective-permute-start(bf16[512,3584]{1,0:T(8,128)(2,1)} %collective-permute-done.1), channel_id=1, source_target_pairs={{0,4},{4,0},{1,5},{5,1},{2,6},{6,2},{3,7},{7,3}} | collective-permute-start | bytes 11010056 | tf_op jit(solution)/shard_map/ppermute | solution.py:16
  1129.0 1458.5 %collective-permute-start.3 = (bf16[512,2560]{0,1:T(8,128)(2,1)}, bf16[512,2560]{0,1:T(8,128)(2,1)}, u32[]{:S(2)}, u32[]{:S(2)}) collective-permute-start(bf16[512,2560]{0,1:T(8,128)(2,1)} %fusion.190), channel_id=1, source_target_pairs={{0,2},{2,0},{1,3},{3,1},{4,6},{6,4},{5,7},{7,5}} | collective-permute-start | bytes 7864328 | tf_op jit(solution)/shard_map/ppermute | solution.py:16
  1191.3 302.9 %collective-permute-start.5 = (bf16[3584,2560]{1,0:T(8,128)(2,1)}, bf16[3584,2560]{1,0:T(8,128)(2,1)}, u32[]{:S(2)}, u32[]{:S(2)}) collective-permute-start(bf16[3584,2560]{1,0:T(8,128)(2,1)} %collective-permute-done), channel_id=1, source_target_pairs={{0,1},{1,0},{2,3},{3,2},{4,5},{5,4},{6,7},{7,6}} | collective-permute-start | bytes 55050248 | tf_op jit(solution)/shard_map/ppermute | solution.py:16
  1316.6 194.8 %collective-permute-start.7 = (bf16[3584,2560]{1,0:T(8,128)(2,1)}, bf16[3584,2560]{1,0:T(8,128)(2,1)}, u32[]{:S(2)}, u32[]{:S(2)}) collective-permute-start(bf16[3584,2560]{1,0:T(8,128)(2,1)} %collective-permute-done.2), channel_id=1, source_target_pairs={{0,1},{1,0},{2,3},{3,2},{4,5},{5,4},{6,7},{7,6}} | collective-permute-start | bytes 55050248 | tf_op jit(solution)/shard_map/ppermute | solution.py:16
  1397.7 699.4 %collective-permute-start.12 = (bf16[512,2560]{0,1:T(8,128)(2,1)}, bf16[512,2560]{0,1:T(8,128)(2,1)}, u32[]{:S(2)}, u32[]{:S(2)}) collective-permute-start(bf16[512,2560]{0,1:T(8,128)(2,1)} %fusion.188), channel_id=1, source_target_pairs={{0,2},{2,0},{1,3},{3,1},{4,6},{6,4},{5,7},{7,5}} | collective-permute-start | bytes 7864328 | tf_op jit(solution)/shard_map/ppermute | solution.py:16
  1494.1 543.1 %collective-permute-start.35 = (bf16[512,2560]{0,1:T(8,128)(2,1)}, bf16[512,2560]{0,1:T(8,128)(2,1)}, u32[]{:S(2)}, u32[]{:S(2)}) collective-permute-start(bf16[512,2560]{0,1:T(8,128)(2,1)} %fusion.176), channel_id=1, source_target_pairs={{0,2},{2,0},{1,3},{3,1},{4,6},{6,4},{5,7},{7,5}} | collective-permute-start | bytes 7864328 | tf_op jit(solution)/shard_map/ppermute | solution.py:16
  1531.0 492.7 %collective-permute-start.32 = (bf16[512,1280]{0,1:T(8,128)(2,1)}, bf16[512,1280]{0,1:T(8,128)(2,1)}, u32[]{:S(2)}, u32[]{:S(2)}) collective-permute-start(bf16[512,1280]{0,1:T(8,128)(2,1)} %slice.223), channel_id=1, source_target_pairs={{0,2},{2,0},{1,3},{3,1},{4,6},{6,4},{5,7},{7,5}} | collective-permute-start | bytes 3932168 | tf_op jit(solution)/shard_map/ppermute | solution.py:16
  1568.5 469.5 %collective-permute-start.36 = (bf16[512,2560]{0,1:T(8,128)(2,1)}, bf16[512,2560]{0,1:T(8,128)(2,1)}, u32[]{:S(2)}, u32[]{:S(2)}) collective-permute-start(bf16[512,2560]{0,1:T(8,128)(2,1)} %fusion.175), channel_id=1, source_target_pairs={{0,2},{2,0},{1,3},{3,1},{4,6},{6,4},{5,7},{7,5}} | collective-permute-start | bytes 7864328 | tf_op jit(solution)/shard_map/ppermute | solution.py:16
  2023.7 232.3 %collective-permute-start.19 = (bf16[512,2560]{0,1:T(8,128)(2,1)}, bf16[512,2560]{0,1:T(8,128)(2,1)}, u32[]{:S(2)}, u32[]{:S(2)}) collective-permute-start(bf16[512,2560]{0,1:T(8,128)(2,1)} %fusion.184), channel_id=1, source_target_pairs={{0,2},{2,0},{1,3},{3,1},{4,6},{6,4},{5,7},{7,5}} | collective-permute-start | bytes 7864328 | tf_op jit(solution)/shard_map/ppermute | solution.py:16
  2037.2 278.8 %collective-permute-start.26 = (bf16[512,2560]{0,1:T(8,128)(2,1)S(1)}, bf16[512,2560]{0,1:T(8,128)(2,1)}, u32[]{:S(2)}, u32[]{:S(2)}) collective-permute-start(bf16[512,2560]{0,1:T(8,128)(2,1)S(1)} %copy-done.5), channel_id=1, source_target_pairs={{0,2},{2,0},{1,3},{3,1},{4,6},{6,4},{5,7},{7,5}} | collective-permute-start | bytes 7864328 | tf_op jit(solution)/shard_map/ppermute | solution.py:16
  2038.0 158.1 %collective-permute-start.13 = (bf16[512,2560]{0,1:T(8,128)(2,1)}, bf16[512,2560]{0,1:T(8,128)(2,1)}, u32[]{:S(2)}, u32[]{:S(2)}) collective-permute-start(bf16[512,2560]{0,1:T(8,128)(2,1)} %fusion.187), channel_id=1, source_target_pairs={{0,2},{2,0},{1,3},{3,1},{4,6},{6,4},{5,7},{7,5}} | collective-permute-start | bytes 7864328 | tf_op jit(solution)/shard_map/ppermute | solution.py:16
  2097.2 159.3 %collective-permute-start.20 = (bf16[512,2560]{0,1:T(8,128)(2,1)}, bf16[512,2560]{0,1:T(8,128)(2,1)}, u32[]{:S(2)}, u32[]{:S(2)}) collective-permute-start(bf16[512,2560]{0,1:T(8,128)(2,1)} %fusion.183), channel_id=1, source_target_pairs={{0,2},{2,0},{1,3},{3,1},{4,6},{6,4},{5,7},{7,5}} | collective-permute-start | bytes 7864328 | tf_op jit(solution)/shard_map/ppermute | solution.py:16
  2256.0 333.5 %collective-permute-start.14 = (f32[512,3584]{1,0:T(8,128)}, f32[512,3584]{1,0:T(8,128)}, u32[]{:S(2)}, u32[]{:S(2)}) collective-permute-start(f32[512,3584]{1,0:T(8,128)} %fusion.14), channel_id=1, source_target_pairs={{0,4},{4,0},{1,5},{5,1},{2,6},{6,2},{3,7},{7,3}} | collective-permute-start | bytes 22020104 | tf_op jit(solution)/shard_map/ppermute | solution.py:16
  2256.5 318.0 %collective-permute-start.37 = (f32[512,3584]{1,0:T(8,128)}, f32[512,3584]{1,0:T(8,128)}, u32[]{:S(2)}, u32[]{:S(2)}) collective-permute-start(f32[512,3584]{1,0:T(8,128)} %fusion.54), channel_id=1, source_target_pairs={{0,4},{4,0},{1,5},{5,1},{2,6},{6,2},{3,7},{7,3}} | collective-permute-start | bytes 22020104 | tf_op jit(solution)/shard_map/ppermute | solution.py:16
  2316.1 272.9 %collective-permute-start.8 = (bf16[512,2560]{0,1:T(8,128)(2,1)}, bf16[512,2560]{0,1:T(8,128)(2,1)}, u32[]{:S(2)}, u32[]{:S(2)}) collective-permute-start(bf16[512,2560]{0,1:T(8,128)(2,1)} %fusion.189), channel_id=1, source_target_pairs={{0,2},{2,0},{1,3},{3,1},{4,6},{6,4},{5,7},{7,5}} | collective-permute-start | bytes 7864328 | tf_op jit(solution)/shard_map/ppermute | solution.py:16
  2316.6 430.8 %collective-permute-start.21 = (f32[512,3584]{1,0:T(8,128)}, f32[512,3584]{1,0:T(8,128)}, u32[]{:S(2)}, u32[]{:S(2)}) collective-permute-start(f32[512,3584]{1,0:T(8,128)} %fusion.30), channel_id=1, source_target_pairs={{0,4},{4,0},{1,5},{5,1},{2,6},{6,2},{3,7},{7,3}} | collective-permute-start | bytes 22020104 | tf_op jit(solution)/shard_map/ppermute | solution.py:16
  2574.4 370.8 %collective-permute-start.33 = (bf16[512,2560]{0,1:T(8,128)(2,1)}, bf16[512,2560]{0,1:T(8,128)(2,1)}, u32[]{:S(2)}, u32[]{:S(2)}) collective-permute-start(bf16[512,2560]{0,1:T(8,128)(2,1)} %fusion.177), channel_id=1, source_target_pairs={{0,2},{2,0},{1,3},{3,1},{4,6},{6,4},{5,7},{7,5}} | collective-permute-start | bytes 7864328 | tf_op jit(solution)/shard_map/ppermute | solution.py:16
  2589.0 157.9 %collective-permute-start.17 = (bf16[512,2560]{0,1:T(8,128)(2,1)}, bf16[512,2560]{0,1:T(8,128)(2,1)}, u32[]{:S(2)}, u32[]{:S(2)}) collective-permute-start(bf16[512,2560]{0,1:T(8,128)(2,1)} %fusion.185), channel_id=1, source_target_pairs={{0,2},{2,0},{1,3},{3,1},{4,6},{6,4},{5,7},{7,5}} | collective-permute-start | bytes 7864328 | tf_op jit(solution)/shard_map/ppermute | solution.py:16
  2589.5 294.3 %collective-permute-start.28 = (f32[512,3584]{1,0:T(8,128)}, f32[512,3584]{1,0:T(8,128)}, u32[]{:S(2)}, u32[]{:S(2)}) collective-permute-start(f32[512,3584]{1,0:T(8,128)} %fusion.46), channel_id=1, source_target_pairs={{0,4},{4,0},{1,5},{5,1},{2,6},{6,2},{3,7},{7,3}} | collective-permute-start | bytes 22020104 | tf_op jit(solution)/shard_map/ppermute | solution.py:16
  2746.8 227.1 %collective-permute-start.38 = (bf16[256,640]{0,1:T(8,128)(2,1)S(1)}, bf16[256,640]{0,1:T(8,128)(2,1)S(1)}, u32[]{:S(2)}, u32[]{:S(2)}) collective-permute-start(bf16[256,640]{0,1:T(8,128)(2,1)S(1)} %copy-done.3), channel_id=1, source_target_pairs={{0,2},{2,0},{1,3},{3,1},{4,6},{6,4},{5,7},{7,5}} | collective-permute-start | bytes 983048 | tf_op jit(solution)/shard_map/ppermute | solution.py:16
  2810.2 158.4 %collective-permute-start.30 = (bf16[256,640]{0,1:T(8,128)(2,1)S(1)}, bf16[256,640]{0,1:T(8,128)(2,1)S(1)}, u32[]{:S(2)}, u32[]{:S(2)}) collective-permute-start(bf16[256,640]{0,1:T(8,128)(2,1)S(1)} %copy-done.4), channel_id=1, source_target_pairs={{0,2},{2,0},{1,3},{3,1},{4,6},{6,4},{5,7},{7,5}} | collective-permute-start | bytes 983048 | tf_op jit(solution)/shard_map/ppermute | solution.py:16
  (17 other events, 1386.0 us)
